TPU v7x, 32 devices: a whole 2x2x4 slice. The times are simulated.
32 devices in a mesh: lon: 16 (over z, y, core), lat: 2 (over x).
Axes of the slice: x: 2, y: 2, z: 4, core: 2. Of those that a mesh axis runs over, the one named last changes fastest.
Arguments:
- fine_members: bfloat16 [32, 64, 256], P(None, 'lon', 'lat'), may hold values from -6 to 6
- coarse_members: bfloat16 [128, 32, 256], P(None, 'lon', 'lat'), may hold values from -6 to 6
- increments: bfloat16 [32, 64, 256], P(None, 'lon', 'lat'), may hold values from -0.59765625 to 0.59765625
- level_weights: float32 [2], replicated, may hold values from 0.5 to 2
Outputs:
- applied: float32 [32, 64, 256], P(None, 'lon', 'lat')
All inputs are finite; a program needn't handle non-finite values.
Results may differ from a plain program's by a relative error of at most 0.0055.
Values may be sent and summed in bfloat16 or wider, within the bound.
A program may use at most 64 MiB of HBM per device.

v0:
```python
import functools

import jax
import jax.numpy as jnp
from jax import lax
from jax.experimental import pallas as pl
from jax.experimental.pallas import tpu as pltpu
from jax.sharding import PartitionSpec as P

MESH = pl.DeviceIdType.MESH
F32, BF16 = jnp.float32, jnp.bfloat16


def profile(distance, extent):
    ratio = distance.astype(F32) / extent
    return jnp.where(jnp.abs(distance) <= extent, 1.0 - 0.75 * ratio * ratio, 0.0)


def iota(shape, dim):
    return lax.broadcasted_iota(jnp.int32, shape, dim)


def kernel(
    sizes, weights_ref, fine_ref, coarse_ref, inc_ref, out_ref,
    w_ref, fine_in, coarse_in, inc_in, wide, own, own_c, west, east, west_cin, east_cin, rim_out, rim_in,
    near, near_inc, own_t, near_rim, rim_inc, taper, rim_taper, refine_rim, acc,
    in_sem, send_sem, recv_sem, rim_send_sem, rim_recv_sem,
):
    n_lon, n_lat, kf, kc, nv, lons, lats = sizes
    halves, reach, lon_reach = lons // 2, lats // 8, lons - 1
    col = kf + nv
    groups = kc // kf
    body = lon_reach * col
    ratio = (kc - 1) / (kf - 1)
    lon, lat = lax.axis_index("lon"), lax.axis_index("lat")
    sides = (lax.rem(lon + n_lon - 1, n_lon), lon, lax.rem(lon + 1, n_lon))
    has = (lat > 0, lat < n_lat - 1)

    barrier = pltpu.get_barrier_semaphore()

    def greet(to_lon, to_lat):
        pl.semaphore_signal(barrier, inc=1, device_id=(to_lon, to_lat), device_id_type=MESH)

    greet(sides[0], lat)
    greet(sides[2], lat)
    for s in range(2):
        @pl.when(has[s])
        def _():
            for t in range(3):
                greet(sides[t], lat + 2 * s - 1)

    loads = [
        pltpu.make_async_copy(src, dst, in_sem.at[n])
        for n, (src, dst) in enumerate(
            ((fine_ref, fine_in), (coarse_ref, coarse_in), (inc_ref, inc_in), (weights_ref, w_ref))
        )
    ]
    for load in loads:
        load.start()

    f_at, c_at, i_at = 0, kf * lons, kf * lons + kc * halves

    loads[0].wait()
    wide[f_at:f_at + kf * lons] = fine_in[...].astype(F32)
    loads[1].wait()
    wide[c_at:c_at + kc * halves] = coarse_in[...].astype(F32)
    loads[2].wait()
    wide[i_at:i_at + nv * lons] = inc_in[...].astype(F32)

    fine_own, inc_own, coarse_own = [], [], []
    for a in range(lons):
        values = wide[pl.ds(f_at + a, kf, stride=lons), :]
        anom = (values - jnp.mean(values, axis=0, keepdims=True)).astype(BF16)
        vectors = wide[pl.ds(i_at + a, nv, stride=lons), :].astype(BF16)
        at = a * col
        own[at:at + kf] = anom
        own[at + kf:at + col] = vectors
        fine_own.append(anom)
        inc_own.append(vectors)
    for c in range(halves):
        values = wide[pl.ds(c_at + c, kc, stride=halves), :]
        own_c[c * kc:(c + 1) * kc] = values.astype(BF16)
        coarse_own.append(values)

    lane = iota((kf, lats), 1)
    packs = (
        [v.astype(F32) for v in fine_own] + [v.astype(F32) for v in inc_own],
        [coarse_own[c][g * kf:(g + 1) * kf] for g in range(groups) for c in range(halves)],
    )
    for part in range(2):
        low = high = jnp.zeros((kf, lats), F32)
        for q, values in enumerate(packs[part]):
            here = (lane // reach) == q
            low = jnp.where(here, pltpu.roll(values, (reach * q) % lats, 1), low)
            high = jnp.where(here, pltpu.roll(values, (reach * (q + 1)) % lats, 1), high)
        rim_out[0, part * kf:(part + 1) * kf] = low.astype(BF16)
        rim_out[1, part * kf:(part + 1) * kf] = high.astype(BF16)

    for s in range(2):
        @pl.when(jnp.logical_not(has[s]))
        def _():
            rim_in[s] = jnp.zeros(rim_in.shape[1:], BF16)

    one = jnp.int32(1)
    pl.semaphore_wait(
        barrier, 2 + 3 * jnp.where(has[0], one, 0) + 3 * jnp.where(has[1], one, 0)
    )

    def send(src, dst, n, towards):
        return pltpu.make_async_remote_copy(
            src_ref=src, dst_ref=dst, send_sem=send_sem.at[n], recv_sem=recv_sem.at[n],
            device_id=(sides[towards], lat), device_id_type=MESH,
        )

    coarse_west = send(own_c, east_cin, 0, 0)
    coarse_east = send(own_c, west_cin, 1, 2)
    rest_west = send(own.at[pl.ds(0, body)], east, 2, 0)
    rest_east = send(own.at[pl.ds(col, body)], west, 3, 2)
    coarse_west.start()
    coarse_east.start()

    def rim_copy(s, t):
        return pltpu.make_async_remote_copy(
            src_ref=rim_out.at[s], dst_ref=rim_in.at[1 - s, 2 - t],
            send_sem=rim_send_sem.at[s, t], recv_sem=rim_recv_sem.at[1 - s, 2 - t],
            device_id=(sides[t], lat + 2 * s - 1), device_id_type=MESH,
        )

    for s in range(2):
        @pl.when(has[s])
        def _():
            for t in (0, 2, 1):
                rim_copy(s, t).start()

    rest_west.start()
    rest_east.start()

    loads[3].wait()
    w_coarse = w_ref[1] / (kc - 1)
    fine_ratio = ratio * w_ref[0] / w_ref[1]
    lat_profile = w_coarse * profile(iota((lats, lats), 0) - iota((lats, lats), 1), reach)
    for d in range(lon_reach + 1):
        taper[d] = lat_profile * (1.0 - 0.75 * (d / lon_reach) * (d / lon_reach))

    block = lons * reach
    shape = (2 * block, lats)
    row, lane = iota(shape, 0), iota(shape, 1)
    side, a_row, i_row = row // block, (row % block) // reach, row % reach
    b_lane, l_lane = lane // reach, lane % reach
    for s in range(2):
        d_lat = i_row - l_lane + reach if s == 0 else reach + l_lane - i_row
        in_lat = jnp.where((side == s) & (b_lane < lons), w_coarse * profile(d_lat, reach), 0.0)
        for t in range(3):
            d_lon = (t - 1) * lons + b_lane - a_row
            n = s * 3 + t
            rim_taper[:, n * lats:(n + 1) * lats] = in_lat * profile(d_lon, lon_reach)

    shape = (2 * lats, lats)
    row, lane = iota(shape, 0), iota(shape, 1)
    place = (row // lats) * halves + (row // reach) % halves
    step = jnp.abs(2 * place - lane // reach)
    weight = jnp.where(step == 0, 1.0, jnp.where(step == 1, 0.5, 0.0))
    weight = jnp.where((row % reach == lane % reach) & (lane < block), weight, 0.0)
    for g in range(groups):
        mine = (row % lats) // (reach * halves) == g
        refine_rim[:, g * lats:(g + 1) * lats] = jnp.where(mine, weight, 0.0).astype(BF16)

    def coarse_parts(refined):
        coarse_anom = refined - jnp.mean(refined, axis=0, keepdims=True)
        pair = refined[:kf]
        paired = pair - jnp.mean(pair, axis=0, keepdims=True)
        return coarse_anom.astype(BF16), paired.astype(BF16)

    def lanes_of(b):
        return slice((b + lon_reach) * lats, (b + lon_reach + 1) * lats)

    def set_near(to, lanes, refined):
        coarse_anom, paired = coarse_parts(refined)
        to[2 * kf:2 * kf + kc, lanes] = coarse_anom
        to[2 * kf + kc:3 * kf + kc, lanes] = paired
        to[3 * kf + kc:, lanes] = paired
        return coarse_anom, paired

    def set_fine(b, fine_anom, vectors):
        near[:kf, lanes_of(b)] = fine_anom
        near[kf:2 * kf, lanes_of(b)] = fine_anom
        near_inc[:, lanes_of(b)] = vectors

    def split(scale, values):
        scaled = scale * values.astype(F32)
        high = scaled.astype(BF16).astype(F32)
        return [high, scaled - high]

    def set_own(a, refined):
        coarse_anom, paired = set_near(near, lanes_of(a), refined)
        set_fine(a, fine_own[a], inc_own[a])
        parts = split(fine_ratio, fine_own[a]) + [coarse_anom.astype(F32)] + split(-ratio, paired)
        own_t[a * lats:(a + 1) * lats] = jnp.concatenate(parts, axis=0).T.astype(BF16)

    def add(b, first, last):
        lanes = lanes_of(b)
        gram = jnp.dot(
            own_t[first * lats:last * lats], near[:, lanes], preferred_element_type=F32
        )
        tapered = jnp.concatenate(
            [
                (gram[(a - first) * lats:(a - first + 1) * lats] * taper[abs(a - b)]).astype(BF16)
                for a in range(first, last)
            ],
            axis=0,
        )
        acc[:, first * lats:last * lats] += lax.dot_general(
            near_inc[:, lanes], tapered, (((1,), (1,)), ((), ())), preferred_element_type=F32
        )

    acc[...] = jnp.zeros_like(acc)
    for a in range(lon_reach):
        left = coarse_own[a // 2]
        set_own(a, left if a % 2 == 0 else 0.5 * (left + coarse_own[a // 2 + 1]))
    for b in range(lon_reach):
        add(b, 0, lon_reach)

    def from_east():
        coarse_west.wait_recv()
        east_c = [east_cin[c * kc:(c + 1) * kc].astype(F32) for c in range(halves)]
        set_own(lon_reach, 0.5 * (coarse_own[halves - 1] + east_c[0]))
        add(lon_reach, 0, lons)
        for b in range(lon_reach):
            add(b, lon_reach, lons)
        for b in range(lon_reach):
            left = east_c[b // 2]
            refined = left if b % 2 == 0 else 0.5 * (left + east_c[b // 2 + 1])
            set_near(near, lanes_of(lons + b), refined)
        rest_west.wait_recv()
        for b in range(lon_reach):
            at = b * col
            set_fine(lons + b, east[at:at + kf], east[at + kf:at + col])
            add(lons + b, b + 1, lons)

    def from_west():
        coarse_east.wait_recv()
        west_c = [west_cin[c * kc:(c + 1) * kc].astype(F32) for c in range(halves)]
        west_c.append(coarse_own[0])
        for b in range(1, lons):
            left = west_c[b // 2]
            refined = left if b % 2 == 0 else 0.5 * (left + west_c[b // 2 + 1])
            set_near(near, lanes_of(b - lons), refined)
        rest_east.wait_recv()
        for b in range(1, lons):
            at = (b - 1) * col
            set_fine(b - lons, west[at:at + kf], west[at + kf:at + col])
            add(b - lons, 0, b)

    is_last = lon == n_lon - 1
    pl.when(jnp.logical_not(is_last))(from_east)
    from_west()
    pl.when(is_last)(from_east)

    for s in range(2):
        @pl.when(has[s])
        def _():
            for t in range(3):
                rim_copy(1 - s, 2 - t).wait_recv()

    pairs = []
    for s in range(2):
        for t in range(3):
            pairs.append(
                jnp.concatenate((rim_in[s, t, kf:], rim_in[s, min(t + 1, 2), kf:]), axis=1)
            )
    refined_rim = jnp.dot(
        jnp.concatenate(pairs, axis=0), refine_rim[...], preferred_element_type=F32
    )
    for s in range(2):
        for t in range(3):
            n = s * 3 + t
            lanes = slice(n * lats, (n + 1) * lats)
            refined = jnp.concatenate(
                [
                    refined_rim[n * kf:(n + 1) * kf, g * lats:(g + 1) * lats]
                    for g in range(groups)
                ],
                axis=0,
            )
            set_near(near_rim, lanes, refined)
            near_rim[:kf, lanes] = rim_in[s, t, :kf]
            near_rim[kf:2 * kf, lanes] = rim_in[s, t, :kf]
            rim_inc[:, lanes] = pltpu.roll(
                rim_in[s, t, :kf].astype(F32), lats - block, 1
            ).astype(BF16)
    own_rim = jnp.concatenate(
        [
            own_t[a * lats + s * (lats - reach):a * lats + s * (lats - reach) + reach]
            for s in range(2)
            for a in range(lons)
        ],
        axis=0,
    )
    gram = jnp.dot(own_rim, near_rim[...], preferred_element_type=F32)
    tapered = (gram * rim_taper[...]).astype(BF16)
    edge = lax.dot_general(
        rim_inc[...], tapered, (((1,), (1,)), ((), ())), preferred_element_type=F32
    )
    lane = iota((nv, lats), 1)
    for a in range(lons):
        low = pltpu.roll(edge, (lats - reach * a) % lats, 1)
        high = pltpu.roll(edge, (2 * lats - reach - block - reach * a) % lats, 1)
        total = acc[:, a * lats:(a + 1) * lats]
        total += jnp.where(lane < reach, low, 0.0) + jnp.where(lane >= lats - reach, high, 0.0)
        out_ref[pl.ds(a, nv, stride=lons), :] = total

    for copy in (coarse_west, coarse_east, rest_west, rest_east):
        copy.wait_send()
    for s in range(2):
        @pl.when(has[s])
        def _():
            for t in range(3):
                rim_copy(s, t).wait_send()


def solution(mesh):
    n_lon, n_lat = mesh.shape["lon"], mesh.shape["lat"]

    def per_device(fine, coarse, inc, weights):
        kf, lons, lats = fine.shape
        kc, halves, _ = coarse.shape
        nv = inc.shape[0]
        members, col, near_lons = 4 * kf + kc, kf + nv, 3 * lons - 2
        body = (lons - 1) * col
        assert nv == kf and 2 * lons * (lats // 8) == lats and kc * halves == 2 * lons * kf
        result = pl.pallas_call(
            functools.partial(kernel, (n_lon, n_lat, kf, kc, nv, lons, lats)),
            out_shape=pltpu.VMEM((nv * lons, lats), F32),
            in_specs=[pl.BlockSpec(memory_space=pl.ANY)] * 4,
            out_specs=pl.BlockSpec(memory_space=pltpu.VMEM),
            scratch_shapes=[
                pltpu.SMEM(weights.shape, F32),
                pltpu.VMEM((kf * lons, lats), BF16),
                pltpu.VMEM((kc * halves, lats), BF16),
                pltpu.VMEM((nv * lons, lats), BF16),
                pltpu.VMEM((col * lons + kc * halves, lats), F32),
                pltpu.VMEM((body + col, lats), BF16),
                pltpu.VMEM((kc * halves, lats), BF16),
                pltpu.VMEM((body, lats), BF16),
                pltpu.VMEM((body, lats), BF16),
                pltpu.VMEM((kc * halves, lats), BF16),
                pltpu.VMEM((kc * halves, lats), BF16),
                pltpu.VMEM((2, 2 * kf, lats), BF16),
                pltpu.VMEM((2, 3, 2 * kf, lats), BF16),
                pltpu.VMEM((members, near_lons * lats), BF16),
                pltpu.VMEM((nv, near_lons * lats), BF16),
                pltpu.VMEM((lons * lats, members), BF16),
                pltpu.VMEM((members, 6 * lats), BF16),
                pltpu.VMEM((nv, 6 * lats), BF16),
                pltpu.VMEM((lons, lats, lats), F32),
                pltpu.VMEM((lats, 6 * lats), F32),
                pltpu.VMEM((2 * lats, (kc // kf) * lats), BF16),
                pltpu.VMEM((nv, lons * lats), F32),
                pltpu.SemaphoreType.DMA((4,)),
                pltpu.SemaphoreType.DMA((4,)),
                pltpu.SemaphoreType.DMA((4,)),
                pltpu.SemaphoreType.DMA((2, 3)),
                pltpu.SemaphoreType.DMA((2, 3)),
            ],
            compiler_params=pltpu.CompilerParams(collective_id=0, has_side_effects=True),
            name="covariance",
        )(
            weights,
            fine.reshape(kf * lons, lats),
            coarse.reshape(kc * halves, lats),
            inc.reshape(nv * lons, lats),
        )
        return result.reshape(nv, lons, lats)

    spec = P(None, "lon", "lat")
    return jax.shard_map(
        per_device, mesh=mesh, in_specs=(spec, spec, spec, P()), out_specs=spec, check_vma=False
    )
```

profile of v0, /device:TPU:0, one launch (start us, length us, event | category | flops | bytes accessed | tf_op | source)
XLA Modules:
  0.0 12.4 jit_solution(7536147849924667589)
XLA Ops:
  0.0 11.7 %covariance.1 = f32[128,128]{1,0:T(8,128)S(1)} custom-call(f32[2]{0:T(128)} %weights_ref.1, bf16[128,128]{1,0:T(8,128)(2,1)} %bitcast.6, bf16[256,128]{1,0:T(8,128)(2,1)} %bitcast.5, bf16[128,128]{1,0:T(8,128)(2,1)} %bitcast.7), custom_call_target="tpu_custom_call" | custom-call | tf_op jit(solution)/shard_map/covariance/pallas_call | solution.py:331
  11.7 0.6 %copy.6 = f32[32,4,128]{2,1,0:T(4,128)} copy(f32[32,4,128]{2,1,0:T(4,128)S(1)} %bitcast.4) | data formatting | bytes 131072
where the time goes:
time: 12.5 us; the launch traced here: 12.4 us
  Pallas kernels  11.7 us (94%)
  local copies, waits for them, and re-layouts  0.63 us (5%)
    pallas_call x1, Pallas kernels, per_device(): pl.pallas_call(functools.partial(kernel, (n_lon, n_lat, kf, kc, nv, lons,...  11.7 us
    unnamed x1, local copies, waits for them, and re-layouts  0.63 us

commit v1 on v0

v1 whole, which is shorter than its diff:
```python
import functools

import jax
import jax.numpy as jnp
from jax import lax
from jax.experimental import pallas as pl
from jax.experimental.pallas import tpu as pltpu
from jax.sharding import PartitionSpec as P

MESH = pl.DeviceIdType.MESH
F32, BF16 = jnp.float32, jnp.bfloat16


def profile(distance, extent):
    ratio = distance.astype(F32) / extent
    return jnp.where(jnp.abs(distance) <= extent, 1.0 - 0.75 * ratio * ratio, 0.0)


def iota(shape, dim):
    return lax.broadcasted_iota(jnp.int32, shape, dim)


def kernel(
    sizes, weights_ref, fine_ref, coarse_ref, inc_ref, out_ref,
    w_ref, fine_in, coarse_in, inc_in, wide, wide_c, west_cin, east_cin, rim_out, rim_in,
    near_f, near_c, near_p, near_i, own_t, taper, rim_taper, refine_rim, acc,
    in_sem, send_sem, recv_sem, rim_send_sem, rim_recv_sem, ok_sem,
):
    n_lon, n_lat, kf, kc, nv, lons, lats = sizes
    halves, reach, lon_reach = lons // 2, lats // 8, lons - 1
    groups = kc // kf
    ratio = (kc - 1) / (kf - 1)
    lon, lat = lax.axis_index("lon"), lax.axis_index("lat")
    sides = (lax.rem(lon + n_lon - 1, n_lon), lon, lax.rem(lon + 1, n_lon))
    has = (lat > 0, lat < n_lat - 1)
    odd = lax.rem(lat, 2) == 1
    even = jnp.logical_not(odd)
    one_side = n_lat == 2
    slots = range(1) if one_side else range(2)

    barrier = pltpu.get_barrier_semaphore()

    loads = [
        pltpu.make_async_copy(src, dst, in_sem.at[n])
        for n, (src, dst) in enumerate(
            ((coarse_ref, coarse_in), (fine_ref, fine_in), (inc_ref, inc_in), (weights_ref, w_ref))
        )
    ]
    for load in loads:
        load.start()

    def greet(to_lon, to_lat):
        pl.semaphore_signal(barrier, inc=1, device_id=(to_lon, to_lat), device_id_type=MESH)

    greet(sides[0], lat)
    greet(sides[2], lat)

    def by_side(do):
        for s in range(2):
            pl.when(has[s])(functools.partial(do, s))

    def send(src, dst, n, towards):
        return pltpu.make_async_remote_copy(
            src_ref=src, dst_ref=dst, send_sem=send_sem.at[n], recv_sem=recv_sem.at[n],
            device_id=(sides[towards], lat), device_id_type=MESH,
        )

    first, past, last = lon_reach, lon_reach + lons, 2 * lon_reach + lons
    to_west, to_east = pl.ds(first, lon_reach), pl.ds(first + 1, lon_reach)
    from_west, from_east = pl.ds(0, lon_reach), pl.ds(past, lon_reach)
    coarse_west = send(coarse_in, east_cin, 0, 0)
    coarse_east = send(coarse_in, west_cin, 1, 2)
    fine_west = send(near_f.at[to_west], near_f.at[from_east], 2, 0)
    fine_east = send(near_f.at[to_east], near_f.at[from_west], 3, 2)
    inc_west = send(near_i.at[to_west], near_i.at[from_east], 4, 0)
    inc_east = send(near_i.at[to_east], near_i.at[from_west], 5, 2)

    def rim_copy(slot, t):
        s, towards = (jnp.where(has[0], 0, 1), 1 - 2 * lat) if one_side else (slot, 2 * slot - 1)
        other = 0 if one_side else 1 - slot
        return pltpu.make_async_remote_copy(
            src_ref=rim_out.at[s], dst_ref=rim_in.at[other, 2 - t],
            send_sem=rim_send_sem.at[slot, t], recv_sem=rim_recv_sem.at[other, 2 - t],
            device_id=(sides[t], lat + towards), device_id_type=MESH,
        )

    def by_slot(do):
        for slot in slots:
            if one_side:
                do(slot)
            else:
                pl.when(has[slot])(functools.partial(do, slot))

    def rims_start(slot):
        for t in (2, 0, 1):
            rim_copy(slot, t).start()

    def rims_arrive(slot):
        for t in range(3):
            rim_copy(slot if one_side else 1 - slot, 2 - t).wait_recv()

    def rims_sent(slot):
        for t in range(3):
            rim_copy(slot, t).wait_send()

    loads[0].wait()

    @pl.when(even)
    def _():
        pl.semaphore_wait(barrier, 2)
        coarse_west.start()
        coarse_east.start()
        by_side(lambda s: greet(lon, lat + 2 * s - 1))

    def columns(source, slot):
        wide_c[slot] = source[...].astype(F32)
        return [wide_c[slot, pl.ds(c, kc, stride=halves), :] for c in range(halves)]

    f_at, i_at = 0, kf * lons
    loads[1].wait()
    wide[f_at:f_at + kf * lons] = fine_in[...].astype(F32)
    loads[2].wait()
    wide[i_at:i_at + nv * lons] = inc_in[...].astype(F32)
    fine_own, inc_own = [], []
    for a in range(lons):
        values = wide[pl.ds(f_at + a, kf, stride=lons), :]
        anom = (values - jnp.mean(values, axis=0, keepdims=True)).astype(BF16)
        vectors = wide[pl.ds(i_at + a, nv, stride=lons), :].astype(BF16)
        near_f[first + a] = anom
        near_i[first + a] = vectors
        fine_own.append(anom)
        inc_own.append(vectors)

    @pl.when(even)
    def _():
        fine_west.start()
        fine_east.start()
        inc_west.start()
        inc_east.start()

    coarse_own = columns(coarse_in, 0)
    lane = iota((kf, lats), 1)
    packs = (
        [v.astype(F32) for v in fine_own] + [v.astype(F32) for v in inc_own],
        [coarse_own[c][g * kf:(g + 1) * kf] for g in range(groups) for c in range(halves)],
    )
    for part in range(2):
        low = high = jnp.zeros((kf, lats), F32)
        for q, values in enumerate(packs[part]):
            here = (lane // reach) == q
            low = jnp.where(here, pltpu.roll(values, (reach * q) % lats, 1), low)
            high = jnp.where(here, pltpu.roll(values, (reach * (q + 1)) % lats, 1), high)
        rim_out[0, part * kf:(part + 1) * kf] = low.astype(BF16)
        rim_out[1, part * kf:(part + 1) * kf] = high.astype(BF16)

    if not one_side:
        for s in slots:
            @pl.when(jnp.logical_not(has[s]))
            def _():
                rim_in[s] = jnp.zeros(rim_in.shape[1:], BF16)

    one = jnp.int32(1)

    @pl.when(odd)
    def _():
        pl.semaphore_wait(barrier, 2 + jnp.where(has[0], one, 0) + jnp.where(has[1], one, 0))
        by_slot(rims_start)
        coarse_west.start()
        coarse_east.start()
        fine_west.start()
        fine_east.start()
        inc_west.start()
        inc_east.start()
        by_side(lambda s: pl.semaphore_signal(
            ok_sem.at[1 - s], inc=1, device_id=(lon, lat + 2 * s - 1), device_id_type=MESH
        ))

    def even_rims():
        @pl.when(even)
        def _():
            by_side(lambda s: pl.semaphore_wait(ok_sem.at[s], 1))
            by_slot(rims_start)

    loads[3].wait()
    w_coarse = w_ref[1] / (kc - 1)
    fine_ratio = ratio * w_ref[0] / w_ref[1]
    lat_profile = w_coarse * profile(iota((lats, lats), 0) - iota((lats, lats), 1), reach)
    for d in range(lon_reach + 1):
        taper[d] = lat_profile * (1.0 - 0.75 * (d / lon_reach) * (d / lon_reach))

    block = lons * reach
    shape = (2 * block, lats)
    row, lane = iota(shape, 0), iota(shape, 1)
    side, a_row, i_row = row // block, (row % block) // reach, row % reach
    b_lane, l_lane = lane // reach, lane % reach
    d_lat = reach + (2 * side - 1) * (l_lane - i_row)
    for slot in slots:
        mine = side == (jnp.where(has[0], 0, 1) if one_side else slot)
        in_lat = jnp.where(mine & (b_lane < lons), w_coarse * profile(d_lat, reach), 0.0)
        for t in range(3):
            d_lon = (t - 1) * lons + b_lane - a_row
            rim_taper[slot, :, t * lats:(t + 1) * lats] = in_lat * profile(d_lon, lon_reach)

    shape = (2 * lats, lats)
    row, lane = iota(shape, 0), iota(shape, 1)
    place = (row // lats) * halves + (row // reach) % halves
    step = jnp.abs(2 * place - lane // reach)
    weight = jnp.where(step == 0, 1.0, jnp.where(step == 1, 0.5, 0.0))
    weight = jnp.where((row % reach == lane % reach) & (lane < block), weight, 0.0)
    for g in range(groups):
        mine = (row % lats) // (reach * halves) == g
        refine_rim[:, g * lats:(g + 1) * lats] = jnp.where(mine, weight, 0.0).astype(BF16)

    def coarse_parts(refined):
        coarse_anom = refined - jnp.mean(refined, axis=0, keepdims=True)
        pair = refined[:kf]
        paired = pair - jnp.mean(pair, axis=0, keepdims=True)
        return coarse_anom.astype(BF16), paired.astype(BF16)

    def set_near(b, refined):
        coarse_anom, paired = coarse_parts(refined)
        near_c[first + b] = coarse_anom
        near_p[first + b] = paired
        return coarse_anom, paired

    def set_own(a, refined):
        coarse_anom, paired = set_near(a, refined)
        parts = [
            fine_ratio * near_f[first + a].astype(F32),
            coarse_anom.astype(F32),
            -ratio * paired.astype(F32),
        ]
        own_t[a * lats:(a + 1) * lats] = jnp.concatenate(parts, axis=0).T.astype(BF16)

    def add(b, lo, hi):
        members = jnp.concatenate([near_f[first + b], near_c[first + b], near_p[first + b]], axis=0)
        gram = jnp.dot(own_t[lo * lats:hi * lats], members, preferred_element_type=F32)
        tapered = jnp.concatenate(
            [
                (gram[(a - lo) * lats:(a - lo + 1) * lats] * taper[abs(a - b)]).astype(BF16)
                for a in range(lo, hi)
            ],
            axis=0,
        )
        acc[:, lo * lats:hi * lats] += lax.dot_general(
            near_i[first + b], tapered, (((1,), (1,)), ((), ())), preferred_element_type=F32
        )

    def middle(cols, b):
        return cols[b // 2] if b % 2 == 0 else 0.5 * (cols[b // 2] + cols[b // 2 + 1])

    acc[...] = jnp.zeros_like(acc)
    for a in range(lon_reach):
        set_own(a, middle(coarse_own, a))
    for b in range(lon_reach):
        add(b, 0, lon_reach)

    def east_coarse():
        coarse_west.wait_recv()
        east_c = columns(east_cin, 1)
        own_last = wide_c[0, pl.ds(halves - 1, kc, stride=halves), :]
        set_own(lon_reach, 0.5 * (own_last + east_c[0]))
        for b in range(lon_reach):
            set_near(lons + b, middle(east_c, b))
        add(lon_reach, 0, lons)
        for b in range(lon_reach):
            add(b, lon_reach, lons)

    def east_arrive():
        fine_west.wait_recv()
        inc_west.wait_recv()

    def east_rest():
        for b in range(lon_reach):
            add(lons + b, b + 1, lons)

    def west_coarse():
        coarse_east.wait_recv()
        west_c = columns(west_cin, 2)
        west_c.append(wide_c[0, pl.ds(0, kc, stride=halves), :])
        for b in range(1, lons):
            set_near(b - lons, middle(west_c, b))

    def west_arrive():
        fine_east.wait_recv()
        inc_east.wait_recv()

    def west_rest():
        for b in range(1, lons):
            add(b - lons, 0, b)

    def rim_members(slot):
        pairs = [
            jnp.concatenate((rim_in[slot, t, kf:], rim_in[slot, min(t + 1, 2), kf:]), axis=1)
            for t in range(3)
        ]
        refined_rim = jnp.dot(
            jnp.concatenate(pairs, axis=0), refine_rim[...], preferred_element_type=F32
        )
        members, vectors = [], []
        for t in range(3):
            refined = jnp.concatenate(
                [
                    refined_rim[t * kf:(t + 1) * kf, g * lats:(g + 1) * lats]
                    for g in range(groups)
                ],
                axis=0,
            )
            coarse_anom, paired = coarse_parts(refined)
            fine_anom = rim_in[slot, t, :kf]
            members.append(jnp.concatenate([fine_anom, coarse_anom, paired], axis=0))
            vectors.append(pltpu.roll(fine_anom.astype(F32), lats - block, 1).astype(BF16))
        return jnp.concatenate(members, axis=1), jnp.concatenate(vectors, axis=1)

    def finish(arrive, rest):
        by_slot(rims_arrive)
        rims = [rim_members(slot) for slot in slots]
        arrive()
        rest()
        own_rim = jnp.concatenate(
            [
                own_t[a * lats + s * (lats - reach):a * lats + s * (lats - reach) + reach]
                for s in range(2)
                for a in range(lons)
            ],
            axis=0,
        )
        edge = None
        for slot in slots:
            members, vectors = rims[slot]
            gram = jnp.dot(own_rim, members, preferred_element_type=F32)
            tapered = (gram * rim_taper[slot]).astype(BF16)
            part = lax.dot_general(
                vectors, tapered, (((1,), (1,)), ((), ())), preferred_element_type=F32
            )
            edge = part if edge is None else edge + part
        lane = iota((nv, lats), 1)
        for a in range(lons):
            low = pltpu.roll(edge, (lats - reach * a) % lats, 1)
            high = pltpu.roll(edge, (2 * lats - reach - block - reach * a) % lats, 1)
            total = acc[:, a * lats:(a + 1) * lats]
            total += jnp.where(lane < reach, low, 0.0) + jnp.where(lane >= lats - reach, high, 0.0)
            out_ref[pl.ds(a, nv, stride=lons), :] = total

    @pl.when(lax.rem(lon, 2) == 0)
    def _():
        east_coarse()
        east_arrive()
        east_rest()
        even_rims()
        west_coarse()
        finish(west_arrive, west_rest)

    @pl.when(lax.rem(lon, 2) == 1)
    def _():
        even_rims()
        west_coarse()
        west_arrive()
        west_rest()
        east_coarse()
        finish(east_arrive, east_rest)

    for copy in (coarse_west, coarse_east, fine_west, fine_east, inc_west, inc_east):
        copy.wait_send()
    by_slot(rims_sent)


def solution(mesh):
    n_lon, n_lat = mesh.shape["lon"], mesh.shape["lat"]

    def per_device(fine, coarse, inc, weights):
        kf, lons, lats = fine.shape
        kc, halves, _ = coarse.shape
        nv = inc.shape[0]
        members, near_lons = 2 * kf + kc, 3 * lons - 2
        slots = 1 if n_lat == 2 else 2
        assert nv == kf and 2 * lons * (lats // 8) == lats and kc * halves == 2 * lons * kf
        assert n_lon % 2 == 0
        result = pl.pallas_call(
            functools.partial(kernel, (n_lon, n_lat, kf, kc, nv, lons, lats)),
            out_shape=pltpu.VMEM((nv * lons, lats), F32),
            in_specs=[pl.BlockSpec(memory_space=pl.ANY)] * 4,
            out_specs=pl.BlockSpec(memory_space=pltpu.VMEM),
            scratch_shapes=[
                pltpu.SMEM(weights.shape, F32),
                pltpu.VMEM((kf * lons, lats), BF16),
                pltpu.VMEM((kc * halves, lats), BF16),
                pltpu.VMEM((nv * lons, lats), BF16),
                pltpu.VMEM(((kf + nv) * lons, lats), F32),
                pltpu.VMEM((3, kc * halves, lats), F32),
                pltpu.VMEM((kc * halves, lats), BF16),
                pltpu.VMEM((kc * halves, lats), BF16),
                pltpu.VMEM((2, 2 * kf, lats), BF16),
                pltpu.VMEM((slots, 3, 2 * kf, lats), BF16),
                pltpu.VMEM((near_lons, kf, lats), BF16),
                pltpu.VMEM((near_lons, kc, lats), BF16),
                pltpu.VMEM((near_lons, kf, lats), BF16),
                pltpu.VMEM((near_lons, nv, lats), BF16),
                pltpu.VMEM((lons * lats, members), BF16),
                pltpu.VMEM((lons, lats, lats), F32),
                pltpu.VMEM((slots, lats, 3 * lats), F32),
                pltpu.VMEM((2 * lats, (kc // kf) * lats), BF16),
                pltpu.VMEM((nv, lons * lats), F32),
                pltpu.SemaphoreType.DMA((4,)),
                pltpu.SemaphoreType.DMA((6,)),
                pltpu.SemaphoreType.DMA((6,)),
                pltpu.SemaphoreType.DMA((slots, 3)),
                pltpu.SemaphoreType.DMA((slots, 3)),
                pltpu.SemaphoreType.REGULAR((2,)),
            ],
            compiler_params=pltpu.CompilerParams(collective_id=0, has_side_effects=True),
            name="covariance",
        )(
            weights,
            fine.reshape(kf * lons, lats),
            coarse.reshape(kc * halves, lats),
            inc.reshape(nv * lons, lats),
        )
        return result.reshape(nv, lons, lats)

    spec = P(None, "lon", "lat")
    return jax.shard_map(
        per_device, mesh=mesh, in_specs=(spec, spec, spec, P()), out_specs=spec, check_vma=False
    )
```

time: 12.5 us -> 11.5 us (0.920)
  Pallas kernels: 11.7 us -> 10.7 us
    pallas_call x1, Pallas kernels: 11.7 us -> 10.7 us  [per_device(): pl.pallas_call(functools.partial(kernel, (n_lon, n_lat, kf, kc, nv, lons,...]
where the time goes in v1:
time: 11.5 us; the launch traced here: 11.4 us
  Pallas kernels  10.7 us (93%)
  local copies, waits for them, and re-layouts  0.63 us (5%)
    pallas_call x1, Pallas kernels, per_device(): pl.pallas_call(functools.partial(kernel, (n_lon, n_lat, kf, kc, nv, lons,...  10.7 us
    unnamed x1, local copies, waits for them, and re-layouts  0.63 us

profile of v1, /device:TPU:0, one launch (start us, length us, event | category | flops | bytes accessed | tf_op | source)
XLA Modules:
  0.0 11.4 jit_solution(8896924763800405029)
XLA Ops:
  0.0 10.7 %covariance.1 = f32[128,128]{1,0:T(8,128)S(1)} custom-call(f32[2]{0:T(128)} %weights_ref.1, bf16[128,128]{1,0:T(8,128)(2,1)} %bitcast.6, bf16[256,128]{1,0:T(8,128)(2,1)} %bitcast.5, bf16[128,128]{1,0:T(8,128)(2,1)} %bitcast.7), custom_call_target="tpu_custom_call" | custom-call | tf_op jit(solution)/shard_map/covariance/pallas_call | solution.py:379
  10.7 0.6 %copy.6 = f32[32,4,128]{2,1,0:T(4,128)} copy(f32[32,4,128]{2,1,0:T(4,128)S(1)} %bitcast.4) | data formatting | bytes 131072

commit v2 on v1

--- a/solution.py
+++ b/solution.py
@@ -23,7 +23,7 @@
 def kernel(
     sizes, weights_ref, fine_ref, coarse_ref, inc_ref, out_ref,
     w_ref, fine_in, coarse_in, inc_in, wide, wide_c, west_cin, east_cin, rim_out, rim_in,
-    near_f, near_c, near_p, near_i, own_t, taper, rim_taper, refine_rim, acc,
+    near_f, near_c, near_p, near_i, own_c, own_r, taper, rim_taper, refine_rim, acc,
     in_sem, send_sem, recv_sem, rim_send_sem, rim_recv_sem, ok_sem,
 ):
     n_lon, n_lat, kf, kc, nv, lons, lats = sizes
@@ -57,7 +57,10 @@
 
     def by_side(do):
         for s in range(2):
-            pl.when(has[s])(functools.partial(do, s))
+            if not one_side:
+                pl.when(has[s])(functools.partial(do, s))
+        if one_side:
+            do(lax.rem(lat + 1, 2))
 
     def send(src, dst, n, towards):
         return pltpu.make_async_remote_copy(
@@ -175,12 +178,6 @@
             ok_sem.at[1 - s], inc=1, device_id=(lon, lat + 2 * s - 1), device_id_type=MESH
         ))
 
-    def even_rims():
-        @pl.when(even)
-        def _():
-            by_side(lambda s: pl.semaphore_wait(ok_sem.at[s], 1))
-            by_slot(rims_start)
-
     loads[3].wait()
     w_coarse = w_ref[1] / (kc - 1)
     fine_ratio = ratio * w_ref[0] / w_ref[1]
@@ -223,71 +220,78 @@
         near_p[first + b] = paired
         return coarse_anom, paired
 
+    def split(scale, values):
+        scaled = scale * values.astype(F32)
+        high = scaled.astype(BF16).astype(F32)
+        return [high, scaled - high]
+
     def set_own(a, refined):
         coarse_anom, paired = set_near(a, refined)
-        parts = [
-            fine_ratio * near_f[first + a].astype(F32),
-            coarse_anom.astype(F32),
-            -ratio * paired.astype(F32),
-        ]
-        own_t[a * lats:(a + 1) * lats] = jnp.concatenate(parts, axis=0).T.astype(BF16)
-
-    def add(b, lo, hi):
-        members = jnp.concatenate([near_f[first + b], near_c[first + b], near_p[first + b]], axis=0)
-        gram = jnp.dot(own_t[lo * lats:hi * lats], members, preferred_element_type=F32)
-        tapered = jnp.concatenate(
-            [
-                (gram[(a - lo) * lats:(a - lo + 1) * lats] * taper[abs(a - b)]).astype(BF16)
-                for a in range(lo, hi)
-            ],
-            axis=0,
-        )
-        acc[:, lo * lats:hi * lats] += lax.dot_general(
-            near_i[first + b], tapered, (((1,), (1,)), ((), ())), preferred_element_type=F32
+        rest = split(fine_ratio, near_f[first + a]) + split(-ratio, paired)
+        own_c[a] = coarse_anom.astype(F32).T.astype(BF16)
+        own_r[a] = jnp.concatenate(rest, axis=0).T.astype(BF16)
+
+    def own_rows(lo, hi):
+        return jnp.concatenate(
+            [jnp.concatenate([own_c[a], own_r[a]], axis=1) for a in range(lo, hi)], axis=0
+        )
+
+    def members(coarse_anom, fine_anom, paired):
+        return jnp.concatenate([coarse_anom, fine_anom, fine_anom, paired, paired], axis=0)
+
+    def tapered_rows(b, lo, hi):
+        at = first + b
+        gram = jnp.dot(
+            own_rows(lo, hi), members(near_c[at], near_f[at], near_p[at]), preferred_element_type=F32
+        )
+        return {
+            a: (gram[(a - lo) * lats:(a - lo + 1) * lats] * taper[abs(a - b)]).astype(BF16)
+            for a in range(lo, hi)
+        }
+
+    def apply(rows, a):
+        near = [b for b in rows if a in rows[b]]
+        vectors = jnp.concatenate([near_i[first + b] for b in near], axis=1)
+        tapered = jnp.concatenate([rows[b][a] for b in near], axis=1)
+        return lax.dot_general(
+            vectors, tapered, (((1,), (1,)), ((), ())), preferred_element_type=F32
         )
 
     def middle(cols, b):
         return cols[b // 2] if b % 2 == 0 else 0.5 * (cols[b // 2] + cols[b // 2 + 1])
 
-    acc[...] = jnp.zeros_like(acc)
     for a in range(lon_reach):
         set_own(a, middle(coarse_own, a))
+    rows = {b: tapered_rows(b, 0, lon_reach) for b in range(lon_reach)}
+    for a in range(lon_reach):
+        acc[a] = apply(rows, a)
+
+    @pl.when(even)
+    def _():
+        by_side(lambda s: pl.semaphore_wait(ok_sem.at[s], 1))
+        by_slot(rims_start)
+
+    coarse_west.wait_recv()
+    east_c = columns(east_cin, 1)
+    set_own(lon_reach, 0.5 * (coarse_own[halves - 1] + east_c[0]))
+    rows = {b: tapered_rows(b, lon_reach, lons) for b in range(lon_reach)}
+    rows[lon_reach] = tapered_rows(lon_reach, 0, lons)
     for b in range(lon_reach):
-        add(b, 0, lon_reach)
-
-    def east_coarse():
-        coarse_west.wait_recv()
-        east_c = columns(east_cin, 1)
-        own_last = wide_c[0, pl.ds(halves - 1, kc, stride=halves), :]
-        set_own(lon_reach, 0.5 * (own_last + east_c[0]))
-        for b in range(lon_reach):
-            set_near(lons + b, middle(east_c, b))
-        add(lon_reach, 0, lons)
-        for b in range(lon_reach):
-            add(b, lon_reach, lons)
-
-    def east_arrive():
-        fine_west.wait_recv()
-        inc_west.wait_recv()
-
-    def east_rest():
-        for b in range(lon_reach):
-            add(lons + b, b + 1, lons)
-
-    def west_coarse():
-        coarse_east.wait_recv()
-        west_c = columns(west_cin, 2)
-        west_c.append(wide_c[0, pl.ds(0, kc, stride=halves), :])
-        for b in range(1, lons):
-            set_near(b - lons, middle(west_c, b))
-
-    def west_arrive():
-        fine_east.wait_recv()
-        inc_east.wait_recv()
-
-    def west_rest():
-        for b in range(1, lons):
-            add(b - lons, 0, b)
+        set_near(lons + b, middle(east_c, b))
+    for a in range(lon_reach):
+        acc[a] += apply(rows, a)
+    acc[lon_reach] = apply(rows, lon_reach)
+    fine_west.wait_recv()
+    inc_west.wait_recv()
+    rows = {lons + b: tapered_rows(lons + b, b + 1, lons) for b in range(lon_reach)}
+    for a in range(1, lons):
+        acc[a] += apply(rows, a)
+
+    coarse_east.wait_recv()
+    west_c = columns(west_cin, 2)
+    west_c.append(coarse_own[0])
+    for b in range(1, lons):
+        set_near(b - lons, middle(west_c, b))
 
     def rim_members(slot):
         pairs = [
@@ -297,7 +301,7 @@
         refined_rim = jnp.dot(
             jnp.concatenate(pairs, axis=0), refine_rim[...], preferred_element_type=F32
         )
-        members, vectors = [], []
+        cells, vectors = [], []
         for t in range(3):
             refined = jnp.concatenate(
                 [
@@ -308,57 +312,42 @@
             )
             coarse_anom, paired = coarse_parts(refined)
             fine_anom = rim_in[slot, t, :kf]
-            members.append(jnp.concatenate([fine_anom, coarse_anom, paired], axis=0))
+            cells.append(members(coarse_anom, fine_anom, paired))
             vectors.append(pltpu.roll(fine_anom.astype(F32), lats - block, 1).astype(BF16))
-        return jnp.concatenate(members, axis=1), jnp.concatenate(vectors, axis=1)
-
-    def finish(arrive, rest):
-        by_slot(rims_arrive)
-        rims = [rim_members(slot) for slot in slots]
-        arrive()
-        rest()
-        own_rim = jnp.concatenate(
-            [
-                own_t[a * lats + s * (lats - reach):a * lats + s * (lats - reach) + reach]
-                for s in range(2)
-                for a in range(lons)
-            ],
-            axis=0,
-        )
-        edge = None
-        for slot in slots:
-            members, vectors = rims[slot]
-            gram = jnp.dot(own_rim, members, preferred_element_type=F32)
-            tapered = (gram * rim_taper[slot]).astype(BF16)
-            part = lax.dot_general(
-                vectors, tapered, (((1,), (1,)), ((), ())), preferred_element_type=F32
+        return jnp.concatenate(cells, axis=1), jnp.concatenate(vectors, axis=1)
+
+    by_slot(rims_arrive)
+    rims = [rim_members(slot) for slot in slots]
+    fine_east.wait_recv()
+    inc_east.wait_recv()
+    rows = {b - lons: tapered_rows(b - lons, 0, b) for b in range(1, lons)}
+    total = [acc[a] + apply(rows, a) for a in range(lon_reach)] + [acc[lon_reach]]
+    own_rim = jnp.concatenate(
+        [
+            jnp.concatenate(
+                [own[a, s * (lats - reach):s * (lats - reach) + reach] for own in (own_c, own_r)],
+                axis=1,
             )
-            edge = part if edge is None else edge + part
-        lane = iota((nv, lats), 1)
-        for a in range(lons):
-            low = pltpu.roll(edge, (lats - reach * a) % lats, 1)
-            high = pltpu.roll(edge, (2 * lats - reach - block - reach * a) % lats, 1)
-            total = acc[:, a * lats:(a + 1) * lats]
-            total += jnp.where(lane < reach, low, 0.0) + jnp.where(lane >= lats - reach, high, 0.0)
-            out_ref[pl.ds(a, nv, stride=lons), :] = total
-
-    @pl.when(lax.rem(lon, 2) == 0)
-    def _():
-        east_coarse()
-        east_arrive()
-        east_rest()
-        even_rims()
-        west_coarse()
-        finish(west_arrive, west_rest)
-
-    @pl.when(lax.rem(lon, 2) == 1)
-    def _():
-        even_rims()
-        west_coarse()
-        west_arrive()
-        west_rest()
-        east_coarse()
-        finish(east_arrive, east_rest)
+            for s in range(2)
+            for a in range(lons)
+        ],
+        axis=0,
+    )
+    edge = None
+    for slot in slots:
+        cells, vectors = rims[slot]
+        gram = jnp.dot(own_rim, cells, preferred_element_type=F32)
+        tapered = (gram * rim_taper[slot]).astype(BF16)
+        part = lax.dot_general(
+            vectors, tapered, (((1,), (1,)), ((), ())), preferred_element_type=F32
+        )
+        edge = part if edge is None else edge + part
+    lane = iota((nv, lats), 1)
+    for a in range(lons):
+        low = pltpu.roll(edge, (lats - reach * a) % lats, 1)
+        high = pltpu.roll(edge, (2 * lats - reach - block - reach * a) % lats, 1)
+        rim = jnp.where(lane < reach, low, 0.0) + jnp.where(lane >= lats - reach, high, 0.0)
+        out_ref[pl.ds(a, nv, stride=lons), :] = total[a] + rim
 
     for copy in (coarse_west, coarse_east, fine_west, fine_east, inc_west, inc_east):
         copy.wait_send()
@@ -372,10 +361,9 @@
         kf, lons, lats = fine.shape
         kc, halves, _ = coarse.shape
         nv = inc.shape[0]
-        members, near_lons = 2 * kf + kc, 3 * lons - 2
+        near_lons = 3 * lons - 2
         slots = 1 if n_lat == 2 else 2
         assert nv == kf and 2 * lons * (lats // 8) == lats and kc * halves == 2 * lons * kf
-        assert n_lon % 2 == 0
         result = pl.pallas_call(
             functools.partial(kernel, (n_lon, n_lat, kf, kc, nv, lons, lats)),
             out_shape=pltpu.VMEM((nv * lons, lats), F32),
@@ -396,11 +384,12 @@
                 pltpu.VMEM((near_lons, kc, lats), BF16),
                 pltpu.VMEM((near_lons, kf, lats), BF16),
                 pltpu.VMEM((near_lons, nv, lats), BF16),
-                pltpu.VMEM((lons * lats, members), BF16),
+                pltpu.VMEM((lons, lats, kc), BF16),
+                pltpu.VMEM((lons, lats, 4 * kf), BF16),
                 pltpu.VMEM((lons, lats, lats), F32),
                 pltpu.VMEM((slots, lats, 3 * lats), F32),
                 pltpu.VMEM((2 * lats, (kc // kf) * lats), BF16),
-                pltpu.VMEM((nv, lons * lats), F32),
+                pltpu.VMEM((lons, nv, lats), F32),
                 pltpu.SemaphoreType.DMA((4,)),
                 pltpu.SemaphoreType.DMA((6,)),
                 pltpu.SemaphoreType.DMA((6,)),

time: 11.5 us -> 11.3 us (0.983)
  Pallas kernels: 10.7 us -> 10.5 us
    pallas_call x1, Pallas kernels: 10.7 us -> 10.5 us  [per_device(): pl.pallas_call(functools.partial(kernel, (n_lon, n_lat, kf, kc, nv, lons,...]
where the time goes in v2:
time: 11.3 us; the launch traced here: 11.1 us
  Pallas kernels  10.5 us (93%)
  local copies, waits for them, and re-layouts  0.63 us (6%)
    pallas_call x1, Pallas kernels, per_device(): pl.pallas_call(functools.partial(kernel, (n_lon, n_lat, kf, kc, nv, lons,...  10.5 us
    unnamed x1, local copies, waits for them, and re-layouts  0.63 us

profile of v2, /device:TPU:0, one launch (start us, length us, event | category | flops | bytes accessed | tf_op | source)
XLA Modules:
  0.0 11.1 jit_solution(13827718374396444263)
XLA Ops:
  0.0 10.5 %covariance.1 = f32[128,128]{1,0:T(8,128)S(1)} custom-call(f32[2]{0:T(128)} %weights_ref.1, bf16[128,128]{1,0:T(8,128)(2,1)} %bitcast.6, bf16[256,128]{1,0:T(8,128)(2,1)} %bitcast.5, bf16[128,128]{1,0:T(8,128)(2,1)} %bitcast.7), custom_call_target="tpu_custom_call" | custom-call | tf_op jit(solution)/shard_map/covariance/pallas_call | solution.py:367
  10.5 0.6 %copy.6 = f32[32,4,128]{2,1,0:T(4,128)} copy(f32[32,4,128]{2,1,0:T(4,128)S(1)} %bitcast.4) | data formatting | bytes 131072

commit v3 on v2

--- a/solution.py
+++ b/solution.py
@@ -23,7 +23,7 @@
 def kernel(
     sizes, weights_ref, fine_ref, coarse_ref, inc_ref, out_ref,
     w_ref, fine_in, coarse_in, inc_in, wide, wide_c, west_cin, east_cin, rim_out, rim_in,
-    near_f, near_c, near_p, near_i, own_c, own_r, taper, rim_taper, refine_rim, acc,
+    near_v, near_c, near_p, own_c, own_r, taper, rim_taper, refine_rim, acc,
     in_sem, send_sem, recv_sem, rim_send_sem, rim_recv_sem, ok_sem,
 ):
     n_lon, n_lat, kf, kc, nv, lons, lats = sizes
@@ -49,12 +49,6 @@
     for load in loads:
         load.start()
 
-    def greet(to_lon, to_lat):
-        pl.semaphore_signal(barrier, inc=1, device_id=(to_lon, to_lat), device_id_type=MESH)
-
-    greet(sides[0], lat)
-    greet(sides[2], lat)
-
     def by_side(do):
         for s in range(2):
             if not one_side:
@@ -62,6 +56,16 @@
         if one_side:
             do(lax.rem(lat + 1, 2))
 
+    def greet(to_lon, to_lat):
+        pl.semaphore_signal(barrier, inc=1, device_id=(to_lon, to_lat), device_id_type=MESH)
+
+    greet(sides[0], lat)
+    greet(sides[2], lat)
+
+    @pl.when(even)
+    def _():
+        by_side(lambda s: [greet(sides[t], lat + 2 * s - 1) for t in (1, 0, 2)] and None)
+
     def send(src, dst, n, towards):
         return pltpu.make_async_remote_copy(
             src_ref=src, dst_ref=dst, send_sem=send_sem.at[n], recv_sem=recv_sem.at[n],
@@ -73,10 +77,8 @@
     from_west, from_east = pl.ds(0, lon_reach), pl.ds(past, lon_reach)
     coarse_west = send(coarse_in, east_cin, 0, 0)
     coarse_east = send(coarse_in, west_cin, 1, 2)
-    fine_west = send(near_f.at[to_west], near_f.at[from_east], 2, 0)
-    fine_east = send(near_f.at[to_east], near_f.at[from_west], 3, 2)
-    inc_west = send(near_i.at[to_west], near_i.at[from_east], 4, 0)
-    inc_east = send(near_i.at[to_east], near_i.at[from_west], 5, 2)
+    rest_west = send(near_v.at[to_west], near_v.at[from_east], 2, 0)
+    rest_east = send(near_v.at[to_east], near_v.at[from_west], 3, 2)
 
     def rim_copy(slot, t):
         s, towards = (jnp.where(has[0], 0, 1), 1 - 2 * lat) if one_side else (slot, 2 * slot - 1)
@@ -84,7 +86,7 @@
         return pltpu.make_async_remote_copy(
             src_ref=rim_out.at[s], dst_ref=rim_in.at[other, 2 - t],
             send_sem=rim_send_sem.at[slot, t], recv_sem=rim_recv_sem.at[other, 2 - t],
-            device_id=(sides[t], lat + towards), device_id_type=MESH,
+            device_id=(lax.rem(lon + n_lon - 1 + t, n_lon), lat + towards), device_id_type=MESH,
         )
 
     def by_slot(do):
@@ -95,7 +97,8 @@
                 pl.when(has[slot])(functools.partial(do, slot))
 
     def rims_start(slot):
-        for t in (2, 0, 1):
+        ahead = lax.rem(lon, 2)
+        for t in (1 + ahead, 2 - ahead, 0):
             rim_copy(slot, t).start()
 
     def rims_arrive(slot):
@@ -113,7 +116,6 @@
         pl.semaphore_wait(barrier, 2)
         coarse_west.start()
         coarse_east.start()
-        by_side(lambda s: greet(lon, lat + 2 * s - 1))
 
     def columns(source, slot):
         wide_c[slot] = source[...].astype(F32)
@@ -129,17 +131,15 @@
         values = wide[pl.ds(f_at + a, kf, stride=lons), :]
         anom = (values - jnp.mean(values, axis=0, keepdims=True)).astype(BF16)
         vectors = wide[pl.ds(i_at + a, nv, stride=lons), :].astype(BF16)
-        near_f[first + a] = anom
-        near_i[first + a] = vectors
+        near_v[first + a, :kf] = anom
+        near_v[first + a, kf:] = vectors
         fine_own.append(anom)
         inc_own.append(vectors)
 
     @pl.when(even)
     def _():
-        fine_west.start()
-        fine_east.start()
-        inc_west.start()
-        inc_east.start()
+        rest_west.start()
+        rest_east.start()
 
     coarse_own = columns(coarse_in, 0)
     lane = iota((kf, lats), 1)
@@ -166,16 +166,14 @@
 
     @pl.when(odd)
     def _():
-        pl.semaphore_wait(barrier, 2 + jnp.where(has[0], one, 0) + jnp.where(has[1], one, 0))
+        pl.semaphore_wait(barrier, 2 + 3 * jnp.where(has[0], one, 0) + 3 * jnp.where(has[1], one, 0))
         by_slot(rims_start)
         coarse_west.start()
         coarse_east.start()
-        fine_west.start()
-        fine_east.start()
-        inc_west.start()
-        inc_east.start()
+        rest_west.start()
+        rest_east.start()
         by_side(lambda s: pl.semaphore_signal(
-            ok_sem.at[1 - s], inc=1, device_id=(lon, lat + 2 * s - 1), device_id_type=MESH
+            ok_sem.at[0 if one_side else 1 - s], inc=1, device_id=(lon, lat + 2 * s - 1), device_id_type=MESH
         ))
 
     loads[3].wait()
@@ -227,7 +225,7 @@
 
     def set_own(a, refined):
         coarse_anom, paired = set_near(a, refined)
-        rest = split(fine_ratio, near_f[first + a]) + split(-ratio, paired)
+        rest = split(fine_ratio, near_v[first + a, :kf]) + split(-ratio, paired)
         own_c[a] = coarse_anom.astype(F32).T.astype(BF16)
         own_r[a] = jnp.concatenate(rest, axis=0).T.astype(BF16)
 
@@ -239,20 +237,24 @@
     def members(coarse_anom, fine_anom, paired):
         return jnp.concatenate([coarse_anom, fine_anom, fine_anom, paired, paired], axis=0)
 
-    def tapered_rows(b, lo, hi):
+    def near(b):
         at = first + b
+        return members(near_c[at], near_v[at, :kf], near_p[at])
+
+    def product(rows, bs, lo, hi):
         gram = jnp.dot(
-            own_rows(lo, hi), members(near_c[at], near_f[at], near_p[at]), preferred_element_type=F32
-        )
-        return {
-            a: (gram[(a - lo) * lats:(a - lo + 1) * lats] * taper[abs(a - b)]).astype(BF16)
-            for a in range(lo, hi)
-        }
+            own_rows(lo, hi), jnp.concatenate([near(b) for b in bs], axis=1),
+            preferred_element_type=F32,
+        )
+        for n, b in enumerate(bs):
+            for a in range(lo, hi):
+                part = gram[(a - lo) * lats:(a - lo + 1) * lats, n * lats:(n + 1) * lats]
+                rows[a, b] = (part * taper[abs(a - b)]).astype(BF16)
 
     def apply(rows, a):
-        near = [b for b in rows if a in rows[b]]
-        vectors = jnp.concatenate([near_i[first + b] for b in near], axis=1)
-        tapered = jnp.concatenate([rows[b][a] for b in near], axis=1)
+        bs = sorted(b for row, b in rows if row == a)
+        vectors = jnp.concatenate([near_v[first + b, kf:] for b in bs], axis=1)
+        tapered = jnp.concatenate([rows[a, b] for b in bs], axis=1)
         return lax.dot_general(
             vectors, tapered, (((1,), (1,)), ((), ())), preferred_element_type=F32
         )
@@ -262,28 +264,34 @@
 
     for a in range(lon_reach):
         set_own(a, middle(coarse_own, a))
-    rows = {b: tapered_rows(b, 0, lon_reach) for b in range(lon_reach)}
+    rows = {}
+    product(rows, tuple(range(lon_reach)), 0, lon_reach)
     for a in range(lon_reach):
         acc[a] = apply(rows, a)
 
     @pl.when(even)
     def _():
-        by_side(lambda s: pl.semaphore_wait(ok_sem.at[s], 1))
+        by_side(lambda s: pl.semaphore_wait(ok_sem.at[0 if one_side else s], 1))
         by_slot(rims_start)
 
     coarse_west.wait_recv()
     east_c = columns(east_cin, 1)
     set_own(lon_reach, 0.5 * (coarse_own[halves - 1] + east_c[0]))
-    rows = {b: tapered_rows(b, lon_reach, lons) for b in range(lon_reach)}
-    rows[lon_reach] = tapered_rows(lon_reach, 0, lons)
+    rows = {}
+    product(rows, tuple(range(lon_reach)), lon_reach, lons)
+    product(rows, (lon_reach,), 0, lons)
     for b in range(lon_reach):
         set_near(lons + b, middle(east_c, b))
     for a in range(lon_reach):
         acc[a] += apply(rows, a)
     acc[lon_reach] = apply(rows, lon_reach)
-    fine_west.wait_recv()
-    inc_west.wait_recv()
-    rows = {lons + b: tapered_rows(lons + b, b + 1, lons) for b in range(lon_reach)}
+    rest_west.wait_recv()
+    rows = {}
+    for b in range(0, lon_reach, 2):
+        pair = tuple(lons + n for n in range(b, min(b + 2, lon_reach)))
+        if len(pair) == 2:
+            product(rows, pair[:1], b + 1, b + 2)
+        product(rows, pair, b + len(pair), lons)
     for a in range(1, lons):
         acc[a] += apply(rows, a)
 
@@ -316,11 +324,15 @@
             vectors.append(pltpu.roll(fine_anom.astype(F32), lats - block, 1).astype(BF16))
         return jnp.concatenate(cells, axis=1), jnp.concatenate(vectors, axis=1)
 
+    rest_east.wait_recv()
     by_slot(rims_arrive)
     rims = [rim_members(slot) for slot in slots]
-    fine_east.wait_recv()
-    inc_east.wait_recv()
-    rows = {b - lons: tapered_rows(b - lons, 0, b) for b in range(1, lons)}
+    rows = {}
+    for b in range(lons - 1, 0, -2):
+        pair = tuple(n - lons for n in range(b, max(b - 2, 0), -1))
+        product(rows, pair, 0, b + 1 - len(pair))
+        if len(pair) == 2:
+            product(rows, pair[:1], b - 1, b)
     total = [acc[a] + apply(rows, a) for a in range(lon_reach)] + [acc[lon_reach]]
     own_rim = jnp.concatenate(
         [
@@ -349,7 +361,7 @@
         rim = jnp.where(lane < reach, low, 0.0) + jnp.where(lane >= lats - reach, high, 0.0)
         out_ref[pl.ds(a, nv, stride=lons), :] = total[a] + rim
 
-    for copy in (coarse_west, coarse_east, fine_west, fine_east, inc_west, inc_east):
+    for copy in (coarse_west, coarse_east, rest_west, rest_east):
         copy.wait_send()
     by_slot(rims_sent)
 
@@ -380,10 +392,9 @@
                 pltpu.VMEM((kc * halves, lats), BF16),
                 pltpu.VMEM((2, 2 * kf, lats), BF16),
                 pltpu.VMEM((slots, 3, 2 * kf, lats), BF16),
-                pltpu.VMEM((near_lons, kf, lats), BF16),
+                pltpu.VMEM((near_lons, kf + nv, lats), BF16),
                 pltpu.VMEM((near_lons, kc, lats), BF16),
                 pltpu.VMEM((near_lons, kf, lats), BF16),
-                pltpu.VMEM((near_lons, nv, lats), BF16),
                 pltpu.VMEM((lons, lats, kc), BF16),
                 pltpu.VMEM((lons, lats, 4 * kf), BF16),
                 pltpu.VMEM((lons, lats, lats), F32),
@@ -391,11 +402,11 @@
                 pltpu.VMEM((2 * lats, (kc // kf) * lats), BF16),
                 pltpu.VMEM((lons, nv, lats), F32),
                 pltpu.SemaphoreType.DMA((4,)),
-                pltpu.SemaphoreType.DMA((6,)),
-                pltpu.SemaphoreType.DMA((6,)),
+                pltpu.SemaphoreType.DMA((4,)),
+                pltpu.SemaphoreType.DMA((4,)),
                 pltpu.SemaphoreType.DMA((slots, 3)),
                 pltpu.SemaphoreType.DMA((slots, 3)),
-                pltpu.SemaphoreType.REGULAR((2,)),
+                pltpu.SemaphoreType.REGULAR((slots,)),
             ],
             compiler_params=pltpu.CompilerParams(collective_id=0, has_side_effects=True),
             name="covariance",

time: 11.3 us -> 10.6 us (0.938)
  Pallas kernels: 10.5 us -> 9.84 us
    pallas_call x1, Pallas kernels: 10.5 us -> 9.84 us  [per_device(): pl.pallas_call(functools.partial(kernel, (n_lon, n_lat, kf, kc, nv, lons,...]
where the time goes in v3:
time: 10.6 us; the launch traced here: 10.5 us
  Pallas kernels  9.84 us (93%)
  local copies, waits for them, and re-layouts  0.63 us (6%)
    pallas_call x1, Pallas kernels, per_device(): pl.pallas_call(functools.partial(kernel, (n_lon, n_lat, kf, kc, nv, lons,...  9.84 us
    unnamed x1, local copies, waits for them, and re-layouts  0.63 us

profile of v3, /device:TPU:0, one launch (start us, length us, event | category | flops | bytes accessed | tf_op | source)
XLA Modules:
  0.0 10.5 jit_solution(10710571033314885037)
XLA Ops:
  0.0 9.8 %covariance.1 = f32[128,128]{1,0:T(8,128)S(1)} custom-call(f32[2]{0:T(128)} %weights_ref.1, bf16[128,128]{1,0:T(8,128)(2,1)} %bitcast.6, bf16[256,128]{1,0:T(8,128)(2,1)} %bitcast.5, bf16[128,128]{1,0:T(8,128)(2,1)} %bitcast.7), custom_call_target="tpu_custom_call" | custom-call | tf_op jit(solution)/shard_map/covariance/pallas_call | solution.py:379
  9.8 0.6 %copy.6 = f32[32,4,128]{2,1,0:T(4,128)} copy(f32[32,4,128]{2,1,0:T(4,128)S(1)} %bitcast.4) | data formatting | bytes 131072

commit v4 on v3

--- a/solution.py
+++ b/solution.py
@@ -23,12 +23,11 @@
 def kernel(
     sizes, weights_ref, fine_ref, coarse_ref, inc_ref, out_ref,
     w_ref, fine_in, coarse_in, inc_in, wide, wide_c, west_cin, east_cin, rim_out, rim_in,
-    near_v, near_c, near_p, own_c, own_r, taper, rim_taper, refine_rim, acc,
+    near_v, near_c, near_p, own_c, own_r, taper, rim_taper, own_rim, acc,
     in_sem, send_sem, recv_sem, rim_send_sem, rim_recv_sem, ok_sem,
 ):
     n_lon, n_lat, kf, kc, nv, lons, lats = sizes
     halves, reach, lon_reach = lons // 2, lats // 8, lons - 1
-    groups = kc // kf
     ratio = (kc - 1) / (kf - 1)
     lon, lat = lax.axis_index("lon"), lax.axis_index("lat")
     sides = (lax.rem(lon + n_lon - 1, n_lon), lon, lax.rem(lon + 1, n_lon))
@@ -81,10 +80,10 @@
     rest_east = send(near_v.at[to_east], near_v.at[from_west], 3, 2)
 
     def rim_copy(slot, t):
-        s, towards = (jnp.where(has[0], 0, 1), 1 - 2 * lat) if one_side else (slot, 2 * slot - 1)
+        towards = 1 - 2 * lat if one_side else 2 * slot - 1
         other = 0 if one_side else 1 - slot
         return pltpu.make_async_remote_copy(
-            src_ref=rim_out.at[s], dst_ref=rim_in.at[other, 2 - t],
+            src_ref=rim_out.at[slot], dst_ref=rim_in.at[other, 2 - t],
             send_sem=rim_send_sem.at[slot, t], recv_sem=rim_recv_sem.at[other, 2 - t],
             device_id=(lax.rem(lon + n_lon - 1 + t, n_lon), lat + towards), device_id_type=MESH,
         )
@@ -142,19 +141,33 @@
         rest_east.start()
 
     coarse_own = columns(coarse_in, 0)
-    lane = iota((kf, lats), 1)
-    packs = (
-        [v.astype(F32) for v in fine_own] + [v.astype(F32) for v in inc_own],
-        [coarse_own[c][g * kf:(g + 1) * kf] for g in range(groups) for c in range(halves)],
-    )
-    for part in range(2):
-        low = high = jnp.zeros((kf, lats), F32)
-        for q, values in enumerate(packs[part]):
-            here = (lane // reach) == q
-            low = jnp.where(here, pltpu.roll(values, (reach * q) % lats, 1), low)
-            high = jnp.where(here, pltpu.roll(values, (reach * (q + 1)) % lats, 1), high)
-        rim_out[0, part * kf:(part + 1) * kf] = low.astype(BF16)
-        rim_out[1, part * kf:(part + 1) * kf] = high.astype(BF16)
+    centred = [v - jnp.mean(v, axis=0, keepdims=True) for v in coarse_own]
+    row, lane = iota((kc, lats), 0), iota((kc, lats), 1)
+    block = lons * reach
+    half = block // 2
+    pad = jnp.zeros((kc - halves * kf, lats), F32)
+    for slot in slots:
+        s = jnp.where(has[0], 0, 1) if one_side else slot
+
+        def strip(values, q):
+            return pltpu.roll(values, lax.rem(reach * (s + q), lats), 1)
+
+        cells = jnp.zeros((kc, lats), F32)
+        for c in range(halves):
+            cells = jnp.where(lane // reach == c, strip(centred[c], c), cells)
+        for e in range(halves):
+            fine = [fine_own[e + halves * h].astype(F32) for h in range(2)]
+            fine = jnp.concatenate(fine + [pad], axis=0)
+            cells = jnp.where(lane // reach == halves + e, strip(fine, halves + e), cells)
+        cells = cells.T
+        low = cells[half:2 * half]
+        lane_v = iota((nv, lats), 1)
+        for a in range(lons):
+            low = jnp.where(
+                lane_v // reach == lons + a, strip(inc_own[a].astype(F32), lons + a), low
+            )
+        rim_out[slot, :half] = cells[:half].astype(BF16)
+        rim_out[slot, half:] = low.astype(BF16)
 
     if not one_side:
         for s in slots:
@@ -183,28 +196,18 @@
     for d in range(lon_reach + 1):
         taper[d] = lat_profile * (1.0 - 0.75 * (d / lon_reach) * (d / lon_reach))
 
-    block = lons * reach
-    shape = (2 * block, lats)
+    shape = (half, lats)
     row, lane = iota(shape, 0), iota(shape, 1)
-    side, a_row, i_row = row // block, (row % block) // reach, row % reach
-    b_lane, l_lane = lane // reach, lane % reach
-    d_lat = reach + (2 * side - 1) * (l_lane - i_row)
+    a_lane, i_lane = lane // (2 * reach), lane % reach
+    side = 1 - (lane // reach) % 2
+    d_lat = reach + (2 * side - 1) * (row % reach - i_lane)
     for slot in slots:
         mine = side == (jnp.where(has[0], 0, 1) if one_side else slot)
-        in_lat = jnp.where(mine & (b_lane < lons), w_coarse * profile(d_lat, reach), 0.0)
-        for t in range(3):
-            d_lon = (t - 1) * lons + b_lane - a_row
-            rim_taper[slot, :, t * lats:(t + 1) * lats] = in_lat * profile(d_lon, lon_reach)
-
-    shape = (2 * lats, lats)
-    row, lane = iota(shape, 0), iota(shape, 1)
-    place = (row // lats) * halves + (row // reach) % halves
-    step = jnp.abs(2 * place - lane // reach)
-    weight = jnp.where(step == 0, 1.0, jnp.where(step == 1, 0.5, 0.0))
-    weight = jnp.where((row % reach == lane % reach) & (lane < block), weight, 0.0)
-    for g in range(groups):
-        mine = (row % lats) // (reach * halves) == g
-        refine_rim[:, g * lats:(g + 1) * lats] = jnp.where(mine, weight, 0.0).astype(BF16)
+        in_lat = jnp.where(mine, w_coarse * profile(d_lat, reach), 0.0)
+        for h in range(2):
+            for t in range(3):
+                d_lon = (t - 1) * lons + halves * h + row // reach - a_lane
+                rim_taper[slot, h, t * half:(t + 1) * half] = in_lat * profile(d_lon, lon_reach)
 
     def coarse_parts(refined):
         coarse_anom = refined - jnp.mean(refined, axis=0, keepdims=True)
@@ -295,38 +298,56 @@
     for a in range(1, lons):
         acc[a] += apply(rows, a)
 
+    c_rows, r_rows = (
+        jnp.concatenate(
+            [own[a, at:at + reach] for a in range(lons) for at in (lats - reach, 0)], axis=0
+        ).astype(F32)
+        for own in (own_c, own_r)
+    )
+    lead = iota((lats, kc), 1) < kf
+    paired = pltpu.roll(r_rows, lats - 2 * kf, 1) + pltpu.roll(r_rows, lats - 3 * kf, 1)
+    c_rows += jnp.where(lead, paired, 0.0)
+    fine_rows = jnp.where(lead, r_rows, 0.0)
+    for h in range(2):
+        own_rim[h, :, :kc] = c_rows.astype(BF16)
+        own_rim[h, :, kc:] = (pltpu.roll(fine_rows, kf, 1) if h else fine_rows).astype(BF16)
+
     coarse_east.wait_recv()
     west_c = columns(west_cin, 2)
     west_c.append(coarse_own[0])
     for b in range(1, lons):
         set_near(b - lons, middle(west_c, b))
 
-    def rim_members(slot):
-        pairs = [
-            jnp.concatenate((rim_in[slot, t, kf:], rim_in[slot, min(t + 1, 2), kf:]), axis=1)
-            for t in range(3)
-        ]
-        refined_rim = jnp.dot(
-            jnp.concatenate(pairs, axis=0), refine_rim[...], preferred_element_type=F32
-        )
-        cells, vectors = [], []
+    def average(x, y):
+        return (0.5 * (x.astype(F32) + y.astype(F32))).astype(BF16)
+
+    def rim_edge(slot):
+        cells = ([], [])
         for t in range(3):
-            refined = jnp.concatenate(
-                [
-                    refined_rim[t * kf:(t + 1) * kf, g * lats:(g + 1) * lats]
-                    for g in range(groups)
-                ],
-                axis=0,
+            west, east = rim_in[slot, t, :reach], rim_in[slot, t, reach:half]
+            beyond = rim_in[slot, min(t + 1, 2), :reach]
+            for h, pair in enumerate(((west, east), (east, beyond))):
+                coarse = jnp.concatenate([pair[0], average(*pair)], axis=0)
+                cells[h].append(jnp.concatenate([coarse, rim_in[slot, t, half:]], axis=1))
+        taps = []
+        for h in range(2):
+            gram = lax.dot_general(
+                jnp.concatenate(cells[h], axis=0), own_rim[h], (((1,), (1,)), ((), ())),
+                preferred_element_type=F32,
             )
-            coarse_anom, paired = coarse_parts(refined)
-            fine_anom = rim_in[slot, t, :kf]
-            cells.append(members(coarse_anom, fine_anom, paired))
-            vectors.append(pltpu.roll(fine_anom.astype(F32), lats - block, 1).astype(BF16))
-        return jnp.concatenate(cells, axis=1), jnp.concatenate(vectors, axis=1)
+            taps.append((gram * rim_taper[slot, h]).astype(BF16))
+        order = [taps[h][t * half:(t + 1) * half] for t in range(3) for h in range(2)]
+        order.append(jnp.zeros((block, lats), BF16))
+        vectors = [rim_in[slot, t, half:].astype(F32) for t in range(3)]
+        lane = iota((nv, lats), 1)
+        first_two = jnp.where(lane < block, pltpu.roll(vectors[0], block, 1), vectors[1])
+        vectors = jnp.concatenate([first_two, pltpu.roll(vectors[2], block, 1)], axis=1)
+        return jnp.dot(
+            vectors.astype(BF16), jnp.concatenate(order, axis=0), preferred_element_type=F32
+        )
 
     rest_east.wait_recv()
     by_slot(rims_arrive)
-    rims = [rim_members(slot) for slot in slots]
     rows = {}
     for b in range(lons - 1, 0, -2):
         pair = tuple(n - lons for n in range(b, max(b - 2, 0), -1))
@@ -334,32 +355,12 @@
         if len(pair) == 2:
             product(rows, pair[:1], b - 1, b)
     total = [acc[a] + apply(rows, a) for a in range(lon_reach)] + [acc[lon_reach]]
-    own_rim = jnp.concatenate(
-        [
-            jnp.concatenate(
-                [own[a, s * (lats - reach):s * (lats - reach) + reach] for own in (own_c, own_r)],
-                axis=1,
-            )
-            for s in range(2)
-            for a in range(lons)
-        ],
-        axis=0,
-    )
-    edge = None
-    for slot in slots:
-        cells, vectors = rims[slot]
-        gram = jnp.dot(own_rim, cells, preferred_element_type=F32)
-        tapered = (gram * rim_taper[slot]).astype(BF16)
-        part = lax.dot_general(
-            vectors, tapered, (((1,), (1,)), ((), ())), preferred_element_type=F32
-        )
-        edge = part if edge is None else edge + part
+    edge = functools.reduce(jnp.add, [rim_edge(slot) for slot in slots])
     lane = iota((nv, lats), 1)
+    at_edge = (lane < reach) | (lane >= lats - reach)
     for a in range(lons):
-        low = pltpu.roll(edge, (lats - reach * a) % lats, 1)
-        high = pltpu.roll(edge, (2 * lats - reach - block - reach * a) % lats, 1)
-        rim = jnp.where(lane < reach, low, 0.0) + jnp.where(lane >= lats - reach, high, 0.0)
-        out_ref[pl.ds(a, nv, stride=lons), :] = total[a] + rim
+        rim = pltpu.roll(edge, (lats - reach - 2 * reach * a) % lats, 1)
+        out_ref[pl.ds(a, nv, stride=lons), :] = total[a] + jnp.where(at_edge, rim, 0.0)
 
     for copy in (coarse_west, coarse_east, rest_west, rest_east):
         copy.wait_send()
@@ -375,7 +376,7 @@
         nv = inc.shape[0]
         near_lons = 3 * lons - 2
         slots = 1 if n_lat == 2 else 2
-        assert nv == kf and 2 * lons * (lats // 8) == lats and kc * halves == 2 * lons * kf
+        assert lons == 4 and nv == kf and lats == kc == 4 * kf
         result = pl.pallas_call(
             functools.partial(kernel, (n_lon, n_lat, kf, kc, nv, lons, lats)),
             out_shape=pltpu.VMEM((nv * lons, lats), F32),
@@ -390,7 +391,7 @@
                 pltpu.VMEM((3, kc * halves, lats), F32),
                 pltpu.VMEM((kc * halves, lats), BF16),
                 pltpu.VMEM((kc * halves, lats), BF16),
-                pltpu.VMEM((2, 2 * kf, lats), BF16),
+                pltpu.VMEM((slots, 2 * kf, lats), BF16),
                 pltpu.VMEM((slots, 3, 2 * kf, lats), BF16),
                 pltpu.VMEM((near_lons, kf + nv, lats), BF16),
                 pltpu.VMEM((near_lons, kc, lats), BF16),
@@ -398,8 +399,8 @@
                 pltpu.VMEM((lons, lats, kc), BF16),
                 pltpu.VMEM((lons, lats, 4 * kf), BF16),
                 pltpu.VMEM((lons, lats, lats), F32),
-                pltpu.VMEM((slots, lats, 3 * lats), F32),
-                pltpu.VMEM((2 * lats, (kc // kf) * lats), BF16),
+                pltpu.VMEM((slots, 2, 3 * kf, lats), F32),
+                pltpu.VMEM((2, lats, 2 * lats), BF16),
                 pltpu.VMEM((lons, nv, lats), F32),
                 pltpu.SemaphoreType.DMA((4,)),
                 pltpu.SemaphoreType.DMA((4,)),

time: 10.6 us -> 10.6 us (level)
  no operation moved by 1% of the time
where the time goes in v4:
time: 10.6 us; the launch traced here: 10.4 us
  Pallas kernels  9.77 us (92%)
  local copies, waits for them, and re-layouts  0.63 us (6%)
    pallas_call x1, Pallas kernels, per_device(): pl.pallas_call(functools.partial(kernel, (n_lon, n_lat, kf, kc, nv, lons,...  9.77 us
    unnamed x1, local copies, waits for them, and re-layouts  0.63 us

profile of v4, /device:TPU:0, one launch (start us, length us, event | category | flops | bytes accessed | tf_op | source)
XLA Modules:
  0.0 10.4 jit_solution(18322872305303797894)
XLA Ops:
  0.0 9.8 %covariance.1 = f32[128,128]{1,0:T(8,128)S(1)} custom-call(f32[2]{0:T(128)} %weights_ref.1, bf16[128,128]{1,0:T(8,128)(2,1)} %bitcast.6, bf16[256,128]{1,0:T(8,128)(2,1)} %bitcast.5, bf16[128,128]{1,0:T(8,128)(2,1)} %bitcast.7), custom_call_target="tpu_custom_call" | custom-call | tf_op jit(solution)/shard_map/covariance/pallas_call | solution.py:380
  9.8 0.6 %copy.6 = f32[32,4,128]{2,1,0:T(4,128)} copy(f32[32,4,128]{2,1,0:T(4,128)S(1)} %bitcast.4) | data formatting | bytes 131072

commit v5 on v4

--- a/solution.py
+++ b/solution.py
@@ -321,7 +321,7 @@
     def average(x, y):
         return (0.5 * (x.astype(F32) + y.astype(F32))).astype(BF16)
 
-    def rim_edge(slot):
+    def rim_taps(slot):
         cells = ([], [])
         for t in range(3):
             west, east = rim_in[slot, t, :reach], rim_in[slot, t, reach:half]
@@ -336,6 +336,9 @@
                 preferred_element_type=F32,
             )
             taps.append((gram * rim_taper[slot, h]).astype(BF16))
+        return taps
+
+    def rim_edge(slot, taps):
         order = [taps[h][t * half:(t + 1) * half] for t in range(3) for h in range(2)]
         order.append(jnp.zeros((block, lats), BF16))
         vectors = [rim_in[slot, t, half:].astype(F32) for t in range(3)]
@@ -348,14 +351,15 @@
 
     rest_east.wait_recv()
     by_slot(rims_arrive)
+    taps = [rim_taps(slot) for slot in slots]
     rows = {}
     for b in range(lons - 1, 0, -2):
         pair = tuple(n - lons for n in range(b, max(b - 2, 0), -1))
         product(rows, pair, 0, b + 1 - len(pair))
         if len(pair) == 2:
             product(rows, pair[:1], b - 1, b)
+    edge = functools.reduce(jnp.add, [rim_edge(slot, taps[slot]) for slot in slots])
     total = [acc[a] + apply(rows, a) for a in range(lon_reach)] + [acc[lon_reach]]
-    edge = functools.reduce(jnp.add, [rim_edge(slot) for slot in slots])
     lane = iota((nv, lats), 1)
     at_edge = (lane < reach) | (lane >= lats - reach)
     for a in range(lons):

time: 10.6 us -> 10.4 us (0.981)
  Pallas kernels: 9.77 us -> 9.56 us
    pallas_call x1, Pallas kernels: 9.77 us -> 9.56 us  [per_device(): pl.pallas_call(functools.partial(kernel, (n_lon, n_lat, kf, kc, nv, lons,...]
where the time goes in v5:
time: 10.4 us; the launch traced here: 10.2 us
  Pallas kernels  9.56 us (92%)
  local copies, waits for them, and re-layouts  0.63 us (6%)
    pallas_call x1, Pallas kernels, per_device(): pl.pallas_call(functools.partial(kernel, (n_lon, n_lat, kf, kc, nv, lons,...  9.56 us
    unnamed x1, local copies, waits for them, and re-layouts  0.63 us

profile of v5, /device:TPU:0, one launch (start us, length us, event | category | flops | bytes accessed | tf_op | source)
XLA Modules:
  0.0 10.2 jit_solution(4154263540037997534)
XLA Ops:
  0.0 9.6 %covariance.1 = f32[128,128]{1,0:T(8,128)S(1)} custom-call(f32[2]{0:T(128)} %weights_ref.1, bf16[128,128]{1,0:T(8,128)(2,1)} %bitcast.6, bf16[256,128]{1,0:T(8,128)(2,1)} %bitcast.5, bf16[128,128]{1,0:T(8,128)(2,1)} %bitcast.7), custom_call_target="tpu_custom_call" | custom-call | tf_op jit(solution)/shard_map/covariance/pallas_call | solution.py:384
  9.6 0.6 %copy.6 = f32[32,4,128]{2,1,0:T(4,128)} copy(f32[32,4,128]{2,1,0:T(4,128)S(1)} %bitcast.4) | data formatting | bytes 131072

commit v6 on v4

--- a/solution.py
+++ b/solution.py
@@ -22,8 +22,8 @@
 
 def kernel(
     sizes, weights_ref, fine_ref, coarse_ref, inc_ref, out_ref,
-    w_ref, fine_in, coarse_in, inc_in, wide, wide_c, west_cin, east_cin, rim_out, rim_in,
-    near_v, near_c, near_p, own_c, own_r, taper, rim_taper, own_rim, acc,
+    w_ref, fine_in, coarse_in, inc_in, wide, wide_c, west_cin, east_cin, turned, rim_in,
+    near_f, near_i, near_c, near_p, own_c, own_r, taper, rim_taper, own_rim, acc,
     in_sem, send_sem, recv_sem, rim_send_sem, rim_recv_sem, ok_sem,
 ):
     n_lon, n_lat, kf, kc, nv, lons, lats = sizes
@@ -65,26 +65,29 @@
     def _():
         by_side(lambda s: [greet(sides[t], lat + 2 * s - 1) for t in (1, 0, 2)] and None)
 
-    def send(src, dst, n, towards):
+    def send(src, dst, sent, arrived, towards):
         return pltpu.make_async_remote_copy(
-            src_ref=src, dst_ref=dst, send_sem=send_sem.at[n], recv_sem=recv_sem.at[n],
+            src_ref=src, dst_ref=dst, send_sem=send_sem.at[sent], recv_sem=recv_sem.at[arrived],
             device_id=(sides[towards], lat), device_id_type=MESH,
         )
 
     first, past, last = lon_reach, lon_reach + lons, 2 * lon_reach + lons
     to_west, to_east = pl.ds(first, lon_reach), pl.ds(first + 1, lon_reach)
     from_west, from_east = pl.ds(0, lon_reach), pl.ds(past, lon_reach)
-    coarse_west = send(coarse_in, east_cin, 0, 0)
-    coarse_east = send(coarse_in, west_cin, 1, 2)
-    rest_west = send(near_v.at[to_west], near_v.at[from_east], 2, 0)
-    rest_east = send(near_v.at[to_east], near_v.at[from_west], 3, 2)
+    coarse_west = send(coarse_in, east_cin, 0, 0, 0)
+    coarse_east = send(coarse_in, west_cin, 0, 1, 2)
+    fine_west = send(near_f.at[to_west], near_f.at[from_east], 1, 2, 0)
+    fine_east = send(near_f.at[to_east], near_f.at[from_west], 1, 3, 2)
+    inc_west = send(near_i.at[to_west], near_i.at[from_east], 1, 2, 0)
+    inc_east = send(near_i.at[to_east], near_i.at[from_west], 1, 4, 2)
 
     def rim_copy(slot, t):
         towards = 1 - 2 * lat if one_side else 2 * slot - 1
         other = 0 if one_side else 1 - slot
+        at = jnp.where(has[0], 0, lats - reach) if one_side else slot * (lats - reach)
         return pltpu.make_async_remote_copy(
-            src_ref=rim_out.at[slot], dst_ref=rim_in.at[other, 2 - t],
-            send_sem=rim_send_sem.at[slot, t], recv_sem=rim_recv_sem.at[other, 2 - t],
+            src_ref=turned.at[:, pl.ds(pl.multiple_of(at, reach), reach)], dst_ref=rim_in.at[other, 2 - t],
+            send_sem=rim_send_sem.at[slot], recv_sem=rim_recv_sem.at[other],
             device_id=(lax.rem(lon + n_lon - 1 + t, n_lon), lat + towards), device_id_type=MESH,
         )
 
@@ -100,13 +103,14 @@
         for t in (1 + ahead, 2 - ahead, 0):
             rim_copy(slot, t).start()
 
+    def drain(ref, sem):
+        pltpu.make_async_copy(ref, ref, sem).wait()
+
     def rims_arrive(slot):
-        for t in range(3):
-            rim_copy(slot if one_side else 1 - slot, 2 - t).wait_recv()
+        drain(rim_in.at[slot], rim_recv_sem.at[slot])
 
     def rims_sent(slot):
-        for t in range(3):
-            rim_copy(slot, t).wait_send()
+        drain(rim_in.at[slot], rim_send_sem.at[slot])
 
     loads[0].wait()
 
@@ -122,52 +126,32 @@
 
     f_at, i_at = 0, kf * lons
     loads[1].wait()
+    loads[2].wait()
+    coarse_own = columns(coarse_in, 0)
     wide[f_at:f_at + kf * lons] = fine_in[...].astype(F32)
-    loads[2].wait()
     wide[i_at:i_at + nv * lons] = inc_in[...].astype(F32)
+    centred = [v - jnp.mean(v, axis=0, keepdims=True) for v in coarse_own]
     fine_own, inc_own = [], []
     for a in range(lons):
         values = wide[pl.ds(f_at + a, kf, stride=lons), :]
         anom = (values - jnp.mean(values, axis=0, keepdims=True)).astype(BF16)
         vectors = wide[pl.ds(i_at + a, nv, stride=lons), :].astype(BF16)
-        near_v[first + a, :kf] = anom
-        near_v[first + a, kf:] = vectors
+        near_f[first + a] = anom
+        near_i[first + a] = vectors
         fine_own.append(anom)
         inc_own.append(vectors)
+    stacks = centred + [
+        jnp.concatenate([v.astype(F32) for v in own], axis=0) for own in (fine_own, inc_own)
+    ]
+    for n, stack in enumerate(stacks):
+        turned[n] = stack.T.astype(BF16)
 
     @pl.when(even)
     def _():
-        rest_west.start()
-        rest_east.start()
-
-    coarse_own = columns(coarse_in, 0)
-    centred = [v - jnp.mean(v, axis=0, keepdims=True) for v in coarse_own]
-    row, lane = iota((kc, lats), 0), iota((kc, lats), 1)
-    block = lons * reach
-    half = block // 2
-    pad = jnp.zeros((kc - halves * kf, lats), F32)
-    for slot in slots:
-        s = jnp.where(has[0], 0, 1) if one_side else slot
-
-        def strip(values, q):
-            return pltpu.roll(values, lax.rem(reach * (s + q), lats), 1)
-
-        cells = jnp.zeros((kc, lats), F32)
-        for c in range(halves):
-            cells = jnp.where(lane // reach == c, strip(centred[c], c), cells)
-        for e in range(halves):
-            fine = [fine_own[e + halves * h].astype(F32) for h in range(2)]
-            fine = jnp.concatenate(fine + [pad], axis=0)
-            cells = jnp.where(lane // reach == halves + e, strip(fine, halves + e), cells)
-        cells = cells.T
-        low = cells[half:2 * half]
-        lane_v = iota((nv, lats), 1)
-        for a in range(lons):
-            low = jnp.where(
-                lane_v // reach == lons + a, strip(inc_own[a].astype(F32), lons + a), low
-            )
-        rim_out[slot, :half] = cells[:half].astype(BF16)
-        rim_out[slot, half:] = low.astype(BF16)
+        fine_west.start()
+        fine_east.start()
+        inc_west.start()
+        inc_east.start()
 
     if not one_side:
         for s in slots:
@@ -183,8 +167,10 @@
         by_slot(rims_start)
         coarse_west.start()
         coarse_east.start()
-        rest_west.start()
-        rest_east.start()
+        fine_west.start()
+        fine_east.start()
+        inc_west.start()
+        inc_east.start()
         by_side(lambda s: pl.semaphore_signal(
             ok_sem.at[0 if one_side else 1 - s], inc=1, device_id=(lon, lat + 2 * s - 1), device_id_type=MESH
         ))
@@ -196,7 +182,7 @@
     for d in range(lon_reach + 1):
         taper[d] = lat_profile * (1.0 - 0.75 * (d / lon_reach) * (d / lon_reach))
 
-    shape = (half, lats)
+    shape = (3 * reach, lats)
     row, lane = iota(shape, 0), iota(shape, 1)
     a_lane, i_lane = lane // (2 * reach), lane % reach
     side = 1 - (lane // reach) % 2
@@ -204,10 +190,9 @@
     for slot in slots:
         mine = side == (jnp.where(has[0], 0, 1) if one_side else slot)
         in_lat = jnp.where(mine, w_coarse * profile(d_lat, reach), 0.0)
-        for h in range(2):
-            for t in range(3):
-                d_lon = (t - 1) * lons + halves * h + row // reach - a_lane
-                rim_taper[slot, h, t * half:(t + 1) * half] = in_lat * profile(d_lon, lon_reach)
+        for b in range(lons):
+            d_lon = (row // reach - 1) * lons + b - a_lane
+            rim_taper[slot, b] = in_lat * profile(d_lon, lon_reach)
 
     def coarse_parts(refined):
         coarse_anom = refined - jnp.mean(refined, axis=0, keepdims=True)
@@ -228,8 +213,11 @@
 
     def set_own(a, refined):
         coarse_anom, paired = set_near(a, refined)
-        rest = split(fine_ratio, near_v[first + a, :kf]) + split(-ratio, paired)
-        own_c[a] = coarse_anom.astype(F32).T.astype(BF16)
+        if a % 2 == 0:
+            own_c[a] = turned[a // 2]
+        else:
+            own_c[a] = coarse_anom.astype(F32).T.astype(BF16)
+        rest = split(fine_ratio, near_f[first + a]) + split(-ratio, paired)
         own_r[a] = jnp.concatenate(rest, axis=0).T.astype(BF16)
 
     def own_rows(lo, hi):
@@ -242,7 +230,7 @@
 
     def near(b):
         at = first + b
-        return members(near_c[at], near_v[at, :kf], near_p[at])
+        return members(near_c[at], near_f[at], near_p[at])
 
     def product(rows, bs, lo, hi):
         gram = jnp.dot(
@@ -256,7 +244,7 @@
 
     def apply(rows, a):
         bs = sorted(b for row, b in rows if row == a)
-        vectors = jnp.concatenate([near_v[first + b, kf:] for b in bs], axis=1)
+        vectors = jnp.concatenate([near_i[first + b] for b in bs], axis=1)
         tapered = jnp.concatenate([rows[a, b] for b in bs], axis=1)
         return lax.dot_general(
             vectors, tapered, (((1,), (1,)), ((), ())), preferred_element_type=F32
@@ -288,7 +276,7 @@
     for a in range(lon_reach):
         acc[a] += apply(rows, a)
     acc[lon_reach] = apply(rows, lon_reach)
-    rest_west.wait_recv()
+    drain(near_f.at[pl.ds(0, 2 * lon_reach)], recv_sem.at[2])
     rows = {}
     for b in range(0, lon_reach, 2):
         pair = tuple(lons + n for n in range(b, min(b + 2, lon_reach)))
@@ -308,9 +296,10 @@
     paired = pltpu.roll(r_rows, lats - 2 * kf, 1) + pltpu.roll(r_rows, lats - 3 * kf, 1)
     c_rows += jnp.where(lead, paired, 0.0)
     fine_rows = jnp.where(lead, r_rows, 0.0)
-    for h in range(2):
-        own_rim[h, :, :kc] = c_rows.astype(BF16)
-        own_rim[h, :, kc:] = (pltpu.roll(fine_rows, kf, 1) if h else fine_rows).astype(BF16)
+    fine_rows += pltpu.roll(fine_rows, kf, 1)
+    fine_rows += pltpu.roll(fine_rows, 2 * kf, 1)
+    own_rim[:, :kc] = c_rows.astype(BF16)
+    own_rim[:, kc:] = fine_rows.astype(BF16)
 
     coarse_east.wait_recv()
     west_c = columns(west_cin, 2)
@@ -321,49 +310,70 @@
     def average(x, y):
         return (0.5 * (x.astype(F32) + y.astype(F32))).astype(BF16)
 
-    def rim_edge(slot):
-        cells = ([], [])
-        for t in range(3):
-            west, east = rim_in[slot, t, :reach], rim_in[slot, t, reach:half]
-            beyond = rim_in[slot, min(t + 1, 2), :reach]
-            for h, pair in enumerate(((west, east), (east, beyond))):
-                coarse = jnp.concatenate([pair[0], average(*pair)], axis=0)
-                cells[h].append(jnp.concatenate([coarse, rim_in[slot, t, half:]], axis=1))
+    def rim_taps(slot):
+        group = iota((reach, lats), 1) // kf
         taps = []
-        for h in range(2):
+        for pair in range(0, lons, 2):
+            cells = []
+            for b in (pair, pair + 1):
+                for t in range(3):
+                    cols = [rim_in[slot, t, c] for c in range(halves)]
+                    cols.append(rim_in[slot, min(t + 1, 2), 0])
+                    coarse = cols[b // 2] if b % 2 == 0 else average(cols[b // 2], cols[b // 2 + 1])
+                    fine = jnp.where(group == b, rim_in[slot, t, halves].astype(F32), 0.0)
+                    cells.append(jnp.concatenate([coarse, fine.astype(BF16)], axis=1))
             gram = lax.dot_general(
-                jnp.concatenate(cells[h], axis=0), own_rim[h], (((1,), (1,)), ((), ())),
+                jnp.concatenate(cells, axis=0), own_rim[...], (((1,), (1,)), ((), ())),
                 preferred_element_type=F32,
             )
-            taps.append((gram * rim_taper[slot, h]).astype(BF16))
-        order = [taps[h][t * half:(t + 1) * half] for t in range(3) for h in range(2)]
-        order.append(jnp.zeros((block, lats), BF16))
-        vectors = [rim_in[slot, t, half:].astype(F32) for t in range(3)]
-        lane = iota((nv, lats), 1)
-        first_two = jnp.where(lane < block, pltpu.roll(vectors[0], block, 1), vectors[1])
-        vectors = jnp.concatenate([first_two, pltpu.roll(vectors[2], block, 1)], axis=1)
-        return jnp.dot(
-            vectors.astype(BF16), jnp.concatenate(order, axis=0), preferred_element_type=F32
-        )
-
-    rest_east.wait_recv()
-    by_slot(rims_arrive)
+            for e in range(2):
+                part = gram[3 * reach * e:3 * reach * (e + 1)]
+                taps.append((part * rim_taper[slot, pair + e]).astype(BF16))
+                taps.append(jnp.zeros((reach, lats), BF16))
+        return jnp.concatenate(taps, axis=0)
+
+    def rim_vectors(slot):
+        cells = [rim_in[slot, t, halves + 1].astype(F32) for t in range(3)]
+        cells = (cells + [jnp.zeros((reach, lats), F32)]) * 2
+        cells = jnp.concatenate(cells, axis=0).T
+        lower = iota((nv, lats), 1) < lats // 2
+        pairs = [
+            jnp.where(lower, cells[b * nv:(b + 1) * nv], cells[(b + 1) * nv:(b + 2) * nv])
+            for b in range(0, lons, 2)
+        ]
+        return jnp.concatenate(pairs, axis=1).astype(BF16)
+
+    drain(wide_c.at[0], send_sem.at[0])
+    drain(turned.at[pl.ds(0, 3)], send_sem.at[1])
+    fine_east.wait_recv()
     rows = {}
     for b in range(lons - 1, 0, -2):
         pair = tuple(n - lons for n in range(b, max(b - 2, 0), -1))
         product(rows, pair, 0, b + 1 - len(pair))
         if len(pair) == 2:
             product(rows, pair[:1], b - 1, b)
+    inc_east.wait_recv()
+    by_slot(rims_arrive)
+    vectors = [rim_vectors(slot) for slot in slots]
+    taps = [rim_taps(slot) for slot in slots]
+    edge = functools.reduce(
+        jnp.add,
+        [
+            jnp.dot(
+                vectors[slot][:, at:at + lats], taps[slot][at:at + lats],
+                preferred_element_type=F32,
+            )
+            for slot in slots
+            for at in (0, lats)
+        ],
+    )
     total = [acc[a] + apply(rows, a) for a in range(lon_reach)] + [acc[lon_reach]]
-    edge = functools.reduce(jnp.add, [rim_edge(slot) for slot in slots])
     lane = iota((nv, lats), 1)
     at_edge = (lane < reach) | (lane >= lats - reach)
     for a in range(lons):
         rim = pltpu.roll(edge, (lats - reach - 2 * reach * a) % lats, 1)
         out_ref[pl.ds(a, nv, stride=lons), :] = total[a] + jnp.where(at_edge, rim, 0.0)
 
-    for copy in (coarse_west, coarse_east, rest_west, rest_east):
-        copy.wait_send()
     by_slot(rims_sent)
 
 
@@ -391,22 +401,23 @@
                 pltpu.VMEM((3, kc * halves, lats), F32),
                 pltpu.VMEM((kc * halves, lats), BF16),
                 pltpu.VMEM((kc * halves, lats), BF16),
-                pltpu.VMEM((slots, 2 * kf, lats), BF16),
-                pltpu.VMEM((slots, 3, 2 * kf, lats), BF16),
-                pltpu.VMEM((near_lons, kf + nv, lats), BF16),
+                pltpu.VMEM((halves + 2, lats, kc), BF16),
+                pltpu.VMEM((slots, 3, halves + 2, lats // 8, kc), BF16),
+                pltpu.VMEM((near_lons, kf, lats), BF16),
+                pltpu.VMEM((near_lons, nv, lats), BF16),
                 pltpu.VMEM((near_lons, kc, lats), BF16),
                 pltpu.VMEM((near_lons, kf, lats), BF16),
                 pltpu.VMEM((lons, lats, kc), BF16),
                 pltpu.VMEM((lons, lats, 4 * kf), BF16),
                 pltpu.VMEM((lons, lats, lats), F32),
-                pltpu.VMEM((slots, 2, 3 * kf, lats), F32),
-                pltpu.VMEM((2, lats, 2 * lats), BF16),
+                pltpu.VMEM((slots, lons, 3 * lats // 8, lats), F32),
+                pltpu.VMEM((lats, 2 * lats), BF16),
                 pltpu.VMEM((lons, nv, lats), F32),
                 pltpu.SemaphoreType.DMA((4,)),
-                pltpu.SemaphoreType.DMA((4,)),
-                pltpu.SemaphoreType.DMA((4,)),
-                pltpu.SemaphoreType.DMA((slots, 3)),
-                pltpu.SemaphoreType.DMA((slots, 3)),
+                pltpu.SemaphoreType.DMA((2,)),
+                pltpu.SemaphoreType.DMA((5,)),
+                pltpu.SemaphoreType.DMA((slots,)),
+                pltpu.SemaphoreType.DMA((slots,)),
                 pltpu.SemaphoreType.REGULAR((slots,)),
             ],
             compiler_params=pltpu.CompilerParams(collective_id=0, has_side_effects=True),

time: 10.6 us -> 10.3 us (0.972)
  Pallas kernels: 9.77 us -> 9.5 us
    pallas_call x1, Pallas kernels: 9.77 us -> 9.5 us  [per_device(): pl.pallas_call(functools.partial(kernel, (n_lon, n_lat, kf, kc, nv, lons,...]
where the time goes in v6:
time: 10.3 us; the launch traced here: 10.1 us
  Pallas kernels  9.5 us (92%)
  local copies, waits for them, and re-layouts  0.63 us (6%)
    pallas_call x1, Pallas kernels, per_device(): pl.pallas_call(functools.partial(kernel, (n_lon, n_lat, kf, kc, nv, lons,...  9.5 us
    unnamed x1, local copies, waits for them, and re-layouts  0.63 us

profile of v6, /device:TPU:0, one launch (start us, length us, event | category | flops | bytes accessed | tf_op | source)
XLA Modules:
  0.0 10.1 jit_solution(8476199078518310786)
XLA Ops:
  0.0 9.5 %covariance.1 = f32[128,128]{1,0:T(8,128)S(1)} custom-call(f32[2]{0:T(128)} %weights_ref.1, bf16[128,128]{1,0:T(8,128)(2,1)} %bitcast.6, bf16[256,128]{1,0:T(8,128)(2,1)} %bitcast.5, bf16[128,128]{1,0:T(8,128)(2,1)} %bitcast.7), custom_call_target="tpu_custom_call" | custom-call | tf_op jit(solution)/shard_map/covariance/pallas_call | solution.py:390
  9.5 0.6 %copy.6 = f32[32,4,128]{2,1,0:T(4,128)} copy(f32[32,4,128]{2,1,0:T(4,128)S(1)} %bitcast.4) | data formatting | bytes 131072

commit v7 on v6

--- a/solution.py
+++ b/solution.py
@@ -117,8 +117,8 @@
     @pl.when(even)
     def _():
         pl.semaphore_wait(barrier, 2)
+        coarse_east.start()
         coarse_west.start()
-        coarse_east.start()
 
     def columns(source, slot):
         wide_c[slot] = source[...].astype(F32)
@@ -141,17 +141,17 @@
         fine_own.append(anom)
         inc_own.append(vectors)
     stacks = centred + [
-        jnp.concatenate([v.astype(F32) for v in own], axis=0) for own in (fine_own, inc_own)
+        jnp.concatenate(own, axis=0) for own in (fine_own, inc_own)
     ]
     for n, stack in enumerate(stacks):
-        turned[n] = stack.T.astype(BF16)
+        turned[n] = stack.astype(BF16).T
 
     @pl.when(even)
     def _():
+        fine_east.start()
+        inc_east.start()
         fine_west.start()
-        fine_east.start()
         inc_west.start()
-        inc_east.start()
 
     if not one_side:
         for s in slots:
@@ -165,12 +165,12 @@
     def _():
         pl.semaphore_wait(barrier, 2 + 3 * jnp.where(has[0], one, 0) + 3 * jnp.where(has[1], one, 0))
         by_slot(rims_start)
+        coarse_east.start()
         coarse_west.start()
-        coarse_east.start()
+        fine_east.start()
+        inc_east.start()
         fine_west.start()
-        fine_east.start()
         inc_west.start()
-        inc_east.start()
         by_side(lambda s: pl.semaphore_signal(
             ok_sem.at[0 if one_side else 1 - s], inc=1, device_id=(lon, lat + 2 * s - 1), device_id_type=MESH
         ))
@@ -216,9 +216,9 @@
         if a % 2 == 0:
             own_c[a] = turned[a // 2]
         else:
-            own_c[a] = coarse_anom.astype(F32).T.astype(BF16)
+            own_c[a] = coarse_anom.T
         rest = split(fine_ratio, near_f[first + a]) + split(-ratio, paired)
-        own_r[a] = jnp.concatenate(rest, axis=0).T.astype(BF16)
+        own_r[a] = jnp.concatenate(rest, axis=0).astype(BF16).T
 
     def own_rows(lo, hi):
         return jnp.concatenate(
@@ -333,9 +333,9 @@
         return jnp.concatenate(taps, axis=0)
 
     def rim_vectors(slot):
-        cells = [rim_in[slot, t, halves + 1].astype(F32) for t in range(3)]
-        cells = (cells + [jnp.zeros((reach, lats), F32)]) * 2
-        cells = jnp.concatenate(cells, axis=0).T
+        cells = [rim_in[slot, t, halves + 1] for t in range(3)]
+        cells = (cells + [jnp.zeros((reach, lats), BF16)]) * 2
+        cells = jnp.concatenate(cells, axis=0).T.astype(F32)
         lower = iota((nv, lats), 1) < lats // 2
         pairs = [
             jnp.where(lower, cells[b * nv:(b + 1) * nv], cells[(b + 1) * nv:(b + 2) * nv])
@@ -352,10 +352,10 @@
         product(rows, pair, 0, b + 1 - len(pair))
         if len(pair) == 2:
             product(rows, pair[:1], b - 1, b)
-    inc_east.wait_recv()
     by_slot(rims_arrive)
     vectors = [rim_vectors(slot) for slot in slots]
     taps = [rim_taps(slot) for slot in slots]
+    inc_east.wait_recv()
     edge = functools.reduce(
         jnp.add,
         [

time: 10.3 us -> 10.3 us (level)
  no operation moved by 1% of the time
where the time goes in v7:
time: 10.3 us; the launch traced here: 10.1 us
  Pallas kernels  9.49 us (92%)
  local copies, waits for them, and re-layouts  0.63 us (6%)
    pallas_call x1, Pallas kernels, per_device(): pl.pallas_call(functools.partial(kernel, (n_lon, n_lat, kf, kc, nv, lons,...  9.49 us
    unnamed x1, local copies, waits for them, and re-layouts  0.63 us

profile of v7, /device:TPU:0, one launch (start us, length us, event | category | flops | bytes accessed | tf_op | source)
XLA Modules:
  0.0 10.1 jit_solution(4997432727819272962)
XLA Ops:
  0.0 9.5 %covariance.1 = f32[128,128]{1,0:T(8,128)S(1)} custom-call(f32[2]{0:T(128)} %weights_ref.1, bf16[128,128]{1,0:T(8,128)(2,1)} %bitcast.6, bf16[256,128]{1,0:T(8,128)(2,1)} %bitcast.5, bf16[128,128]{1,0:T(8,128)(2,1)} %bitcast.7), custom_call_target="tpu_custom_call" | custom-call | tf_op jit(solution)/shard_map/covariance/pallas_call | solution.py:390
  9.5 0.6 %copy.6 = f32[32,4,128]{2,1,0:T(4,128)} copy(f32[32,4,128]{2,1,0:T(4,128)S(1)} %bitcast.4) | data formatting | bytes 131072

commit v8 on v7

--- a/solution.py
+++ b/solution.py
@@ -41,8 +41,9 @@
 
     loads = [
         pltpu.make_async_copy(src, dst, in_sem.at[n])
-        for n, (src, dst) in enumerate(
-            ((coarse_ref, coarse_in), (fine_ref, fine_in), (inc_ref, inc_in), (weights_ref, w_ref))
+        for n, src, dst in (
+            (0, coarse_ref, coarse_in), (1, fine_ref, fine_in), (1, inc_ref, inc_in),
+            (2, weights_ref, w_ref),
         )
     ]
     for load in loads:
@@ -125,8 +126,7 @@
         return [wide_c[slot, pl.ds(c, kc, stride=halves), :] for c in range(halves)]
 
     f_at, i_at = 0, kf * lons
-    loads[1].wait()
-    loads[2].wait()
+    drain(turned.at[pl.ds(0, 2)], in_sem.at[1])
     coarse_own = columns(coarse_in, 0)
     wide[f_at:f_at + kf * lons] = fine_in[...].astype(F32)
     wide[i_at:i_at + nv * lons] = inc_in[...].astype(F32)
@@ -314,9 +314,12 @@
         group = iota((reach, lats), 1) // kf
         taps = []
         for pair in range(0, lons, 2):
-            cells = []
+            cells, places = [], []
             for b in (pair, pair + 1):
                 for t in range(3):
+                    if (t, b) in ((0, 0), (2, lons - 1)):
+                        continue
+                    places.append((b, t))
                     cols = [rim_in[slot, t, c] for c in range(halves)]
                     cols.append(rim_in[slot, min(t + 1, 2), 0])
                     coarse = cols[b // 2] if b % 2 == 0 else average(cols[b // 2], cols[b // 2 + 1])
@@ -326,10 +329,14 @@
                 jnp.concatenate(cells, axis=0), own_rim[...], (((1,), (1,)), ((), ())),
                 preferred_element_type=F32,
             )
-            for e in range(2):
-                part = gram[3 * reach * e:3 * reach * (e + 1)]
-                taps.append((part * rim_taper[slot, pair + e]).astype(BF16))
-                taps.append(jnp.zeros((reach, lats), BF16))
+            for b in (pair, pair + 1):
+                for t in range(4):
+                    if (b, t) not in places:
+                        taps.append(jnp.zeros((reach, lats), BF16))
+                        continue
+                    at = reach * places.index((b, t))
+                    weight = rim_taper[slot, b, t * reach:(t + 1) * reach]
+                    taps.append((gram[at:at + reach] * weight).astype(BF16))
         return jnp.concatenate(taps, axis=0)
 
     def rim_vectors(slot):
@@ -413,7 +420,7 @@
                 pltpu.VMEM((slots, lons, 3 * lats // 8, lats), F32),
                 pltpu.VMEM((lats, 2 * lats), BF16),
                 pltpu.VMEM((lons, nv, lats), F32),
-                pltpu.SemaphoreType.DMA((4,)),
+                pltpu.SemaphoreType.DMA((3,)),
                 pltpu.SemaphoreType.DMA((2,)),
                 pltpu.SemaphoreType.DMA((5,)),
                 pltpu.SemaphoreType.DMA((slots,)),

time: 10.3 us -> 10.3 us (level)
  no operation moved by 1% of the time
where the time goes in v8:
time: 10.3 us; the launch traced here: 10.1 us
  Pallas kernels  9.48 us (92%)
  local copies, waits for them, and re-layouts  0.63 us (6%)
    pallas_call x1, Pallas kernels, per_device(): pl.pallas_call(functools.partial(kernel, (n_lon, n_lat, kf, kc, nv, lons,...  9.48 us
    unnamed x1, local copies, waits for them, and re-layouts  0.63 us

profile of v8, /device:TPU:0, one launch (start us, length us, event | category | flops | bytes accessed | tf_op | source)
XLA Modules:
  0.0 10.1 jit_solution(8720861109111017825)
XLA Ops:
  0.0 9.5 %covariance.1 = f32[128,128]{1,0:T(8,128)S(1)} custom-call(f32[2]{0:T(128)} %weights_ref.1, bf16[128,128]{1,0:T(8,128)(2,1)} %bitcast.6, bf16[256,128]{1,0:T(8,128)(2,1)} %bitcast.5, bf16[128,128]{1,0:T(8,128)(2,1)} %bitcast.7), custom_call_target="tpu_custom_call" | custom-call | tf_op jit(solution)/shard_map/covariance/pallas_call | solution.py:397
  9.5 0.6 %copy.6 = f32[32,4,128]{2,1,0:T(4,128)} copy(f32[32,4,128]{2,1,0:T(4,128)S(1)} %bitcast.4) | data formatting | bytes 131072
